TPU v7x, 32 devices: a 4x4x1 block of a 4x4x8 slice. The times are simulated.
32 devices in a mesh: dp: 1 (over z), m1: 4 (over y), m2: 8 (over x, core).
Axes of the slice: x: 4, y: 4, z: 1, core: 2. Of those that a mesh axis runs over, the one named last changes fastest.
The devices are a block of a 4x4x8 slice.
Arguments:
- x: bfloat16 [32, 256, 4096], P('dp', None, 'm1')
- ln_scale: float32 [4096], replicated
- qn_scale: float32 [128], replicated
- kn_scale: float32 [128], replicated
- w_qkv: bfloat16 [4096, 3, 4096], P('m1', None, 'm2')
- w_up: bfloat16 [4096, 16384], P('m1', 'm2')
- b_up: float32 [16384], P('m2')
- w_o: bfloat16 [4096, 4096], P('m2', 'm1')
- w_down: bfloat16 [16384, 4096], P('m2', 'm1')
- b_out: float32 [4096], P('m1')
Outputs:
- output: bfloat16 [32, 256, 4096], P('dp', None, 'm1')
All inputs are finite; a program needn't handle non-finite values.
Results may differ from a plain program's by a relative error of at most 0.0111303.
Values are sent between devices in bfloat16 or wider.
A program may use at most 768 MiB of HBM per device.

v0:
```python
import jax
import jax.numpy as jnp
from jax import lax
from jax.sharding import PartitionSpec as P

LN_EPS = 1e-6


def layer_norm(values, scale):
    mean = jnp.mean(values, axis=-1, keepdims=True)
    centered = values - mean
    variance = jnp.mean(centered * centered, axis=-1, keepdims=True)
    return centered * lax.rsqrt(variance + LN_EPS) * scale


def solution(mesh):
    group_m1 = mesh.shape['m1']

    def local_layer(x_blk, ln_scale, qn_scale, kn_scale, w_qkv, w_up, b_up, w_o, w_down, b_out):
        batch, patches, dim_local = x_blk.shape
        model_dim = dim_local * group_m1
        head_dim = qn_scale.shape[0]
        heads_local = w_qkv.shape[2] // head_dim
        scale_local = lax.dynamic_slice_in_dim(ln_scale, lax.axis_index('m1') * dim_local, dim_local)
        x_wide = x_blk.astype(jnp.float32)
        moments = jnp.stack([jnp.sum(x_wide, axis=-1), jnp.sum(x_wide * x_wide, axis=-1)])
        moments = lax.psum(moments, 'm1')
        mean = moments[0][..., None] / model_dim
        variance = moments[1][..., None] / model_dim - mean * mean
        normed = ((x_wide - mean) * lax.rsqrt(variance + LN_EPS) * scale_local).astype(jnp.bfloat16)
        qkv_part = jnp.einsum('bnd,dtc->bntc', normed, w_qkv, preferred_element_type=jnp.float32).astype(jnp.bfloat16)
        up_part = jnp.einsum('bnd,df->bnf', normed, w_up, preferred_element_type=jnp.float32).astype(jnp.bfloat16)
        proj_qkv, up_in = lax.psum((qkv_part, up_part), 'm1')
        proj_qkv = proj_qkv.reshape(batch, patches, 3, heads_local, head_dim)
        queries = layer_norm(proj_qkv[:, :, 0].astype(jnp.float32), qn_scale).astype(jnp.bfloat16)
        keys = layer_norm(proj_qkv[:, :, 1].astype(jnp.float32), kn_scale).astype(jnp.bfloat16)
        scores = jnp.einsum('bnhd,bmhd->bhnm', queries, keys, preferred_element_type=jnp.float32) * head_dim ** -0.5
        attn_probs = jax.nn.softmax(scores, axis=-1).astype(jnp.bfloat16)
        attended = jnp.einsum('bhnm,bmhd->bnhd', attn_probs, proj_qkv[:, :, 2], preferred_element_type=jnp.float32).astype(jnp.bfloat16)
        hidden = jax.nn.gelu(up_in.astype(jnp.float32) + b_up, approximate=False).astype(jnp.bfloat16)
        out_part = jnp.einsum('bnhd,hde->bne', attended, w_o.reshape(heads_local, head_dim, dim_local), preferred_element_type=jnp.float32)
        out_part = out_part + jnp.einsum('bnf,fe->bne', hidden, w_down, preferred_element_type=jnp.float32)
        mixed_sum = lax.psum(out_part.astype(jnp.bfloat16), 'm2')
        return (x_wide + mixed_sum.astype(jnp.float32) + b_out).astype(jnp.bfloat16)

    return jax.shard_map(local_layer, mesh=mesh, in_specs=(P('dp', None, 'm1'), P(), P(), P(), P('m1', None, 'm2'), P('m1', 'm2'), P('m2'), P('m2', 'm1'), P('m2', 'm1'), P('m1')), out_specs=P('dp', None, 'm1'), check_vma=False)
```

profile of v0, /device:TPU:97, one launch (start us, length us, event | category | flops | bytes accessed | tf_op | source)
XLA Modules:
  0.0 1652.8 jit_solution(3643145273191557336)
XLA Ops:
  6.5 0.0 copy-start
  6.6 0.0 all-reduce.5.cloned.1.call-start
  6.6 8.0 convert_reduce_fusion
  14.5 0.6 pad_maximum_fusion
  15.2 0.1 all-reduce.5.cloned.1.call-update
  15.2 0.1 all-reduce.9.cloned.1.call-start
  15.3 0.7 dynamic_slice.3
  16.0 37.4 %all-reduce.5.cloned.1.call-done = f32[2,32,256]{2,1,0:T(8,128)} async-done(((f32[2,32,256]{2,1,0:T(8,128)}), f32[2,32,256]{2,1,0:T(8,128)}) %all-reduce.5.cloned.1.call-update) | async-done | bytes 65552 | tf_op jit(solution)/shard_map/psum | solution.py:27
  53.4 0.8 fusion.69
  54.2 0.8 fusion.70
  55.0 0.0 copy-done
  55.0 33.1 %fusion.42 = bf16[32,256,3,512]{3,1,2,0:T(8,128)(2,1)} fusion(bf16[32,256,1024]{2,1,0:T(8,128)(2,1)} %param.10, f32[1024]{0:T(1024)S(1)} %dynamic_slice.3, f32[32,256]{1,0:T(8,128)S(1)} %fusion.69, f32[32,256]{1,0:T(8,128)S(1)} %fusion.70, bf16[1024,3,512]{2,0,1:T(8,128)(2,1)S(1)} %copy-done), kind=kOutput, calls=%fused_computation.61 | convolution fusion | flops 25824329728 | bytes 45158400 | tf_op jit(solution)/shard_map/bnd,dtc->bntc/dot_general | solution.py:31
  88.1 34.9 %reshape.68 = bf16[32,256,3,4,128]{4,3,1,2,0:T(4,128)(2,1)} reshape(bf16[32,256,3,512]{3,1,2,0:T(8,128)(2,1)} %fusion.42) | data formatting | bytes 50331648 | tf_op jit(solution)/shard_map/reshape | solution.py:34
  123.0 22.5 %copy.11 = bf16[32,256,3,4,128]{4,1,3,0,2:T(8,128)(2,1)} copy(bf16[32,256,3,4,128]{4,3,1,2,0:T(4,128)(2,1)} %reshape.68) | data formatting | bytes 50331648 | tf_op jit(solution)/shard_map/reshape | solution.py:34
  145.5 43.5 %convolution_convert_fusion = bf16[32,256,2048]{2,1,0:T(8,128)(2,1)} fusion(bf16[32,256,1024]{2,1,0:T(8,128)(2,1)} %param.10, f32[1024]{0:T(1024)S(1)} %dynamic_slice.3, f32[32,256]{1,0:T(8,128)S(1)} %fusion.69, f32[32,256]{1,0:T(8,128)S(1)} %fusion.70, bf16[1024,2048]{1,0:T(8,128)(2,1)} %param.15), kind=kOutput, calls=%fused_computation.44 | convolution fusion | flops 34418458624 | bytes 54595584 | tf_op jit(solution)/shard_map/bnd,df->bnf/dot_general | solution.py:32
  189.0 0.0 copy-start.2
  189.0 0.0 copy-start.3
  189.0 0.1 all-reduce.9.cloned.1.call-update
  189.1 0.1 all-reduce.7.cloned.1.call-start
  189.2 966.6 %all-reduce.9.cloned.1.call-done = (bf16[32,256,3,4,128]{4,1,3,0,2:T(8,128)(2,1)}, bf16[32,256,2048]{2,1,0:T(8,128)(2,1)}) async-done(((bf16[32,256,3,4,128]{4,1,3,0,2:T(8,128)(2,1)}, bf16[32,256,2048]{2,1,0:T(8,128)(2,1)}), (bf16[32,256,3,4,128]{4,1,3,0,2:T(8,128)(2,1)}, bf16[32,256,2048]{2,1,0:T(8,128)(2,1)})) %all-reduce.9.cloned.1.call-update) | async-done | bytes 58720272 | tf_op jit(solution)/shard_map/psum | solution.py:33
  1155.8 8.7 convert_reduce_fusion.2
  1164.5 0.1 broadcast_multiply_fusion
  1164.6 20.3 %fusion.29 = (f32[32,256,4]{1,2,0:T(4,128)S(1)}, f32[32,256,4]{1,2,0:T(4,128)S(1)}) fusion(f32[32,256,4]{1,2,0:T(4,128)S(1)} %get-tuple-element.16, bf16[32,256,3,4,128]{4,1,3,0,2:T(8,128)(2,1)} %get-tuple-element.11, f32[32,256,4]{1,2,0:T(4,128)S(1)} %get-tuple-element.15), kind=kLoop, calls=%fused_computation.48 | loop fusion | flops 33488896 | bytes 17301504 | tf_op jit(solution)/shard_map/reduce_sum | solution.py:12
  1184.9 0.1 add_rsqrt_fusion.1
  1184.9 0.1 add_rsqrt_fusion
  1185.0 0.0 copy-done.2
  1185.0 0.0 copy-done.3
  1185.0 23.6 %fusion.49 = f32[32,4,256,256]{2,3,1,0:T(8,128)} fusion(f32[128]{0:T(128)S(1)} %copy-done.2, f32[32,256,4]{1,2,0:T(4,128)S(1)} %add_rsqrt_fusion, f32[32,256,4]{1,2,0:T(4,128)S(1)} %get-tuple-element.15, f32[128]{0:T(128)S(1)} %copy-done.3, f32[32,256,4]{1,2,0:T(4,128)S(1)} %add_rsqrt_fusion.1, f32[32,256,4]{1,2,0:T(4,128)S(1)} %get-tuple-element.16, ...), kind=kOutput, calls=%fused_computation.62 | convolution fusion | flops 2189426688 | bytes 50856960 | tf_op jit(solution)/shard_map/bnhd,bmhd->bhnm/dot_general | solution.py:37
  1208.6 0.0 copy-start.5
  1208.6 34.9 %fusion.102 = (f32[32,4,256]{2,1,0:T(4,128)S(1)}, f32[32,4,256,256]{2,3,1,0:T(8,128)}) fusion(f32[32,4,256,256]{2,3,1,0:T(8,128)} %fusion.49), kind=kOutput, calls=%fused_computation.121 | output fusion | flops 33554688 | bytes 67239936 | tf_op jit(solution)/shard_map/sub | solution.py:38
  1243.5 0.0 copy-done.5
  1243.5 0.0 copy-start.6
  1243.5 27.9 %fusion.52 = f32[32,256,1024,1]{2,1,3,0:T(8,128)} fusion(bf16[4,128,1024,1]{2,1,0,3:T(8,128)(2,1)S(1)} %bitcast.94, f32[32,4,256,256]{2,3,1,0:T(8,128)} %get-tuple-element.14, f32[32,4,256]{2,1,0:T(4,128)S(1)} %get-tuple-element.13, bf16[32,256,3,4,128]{4,1,3,0,2:T(8,128)(2,1)} %get-tuple-element.11), kind=kOutput, calls=%fused_computation.64 | convolution fusion | flops 10758389760 | bytes 76677120 | tf_op jit(solution)/shard_map/bnhd,hde->bne/dot_general | solution.py:41
  1271.4 0.0 copy-done.6
  1271.4 0.0 copy-start.4
  1271.4 177.2 %fusion.20 = bf16[32,256,1024]{2,1,0:T(8,128)(2,1)} fusion(f32[32,256,1024,1]{2,1,3,0:T(8,128)} %fusion.52, bf16[32,256,2048]{2,1,0:T(8,128)(2,1)} %get-tuple-element.12, f32[2048]{0:T(1024)S(1)} %copy-done.6, bf16[2048,1024]{1,0:T(8,128)(2,1)} %param.18), kind=kOutput, calls=%fused_computation.34 | convolution fusion | flops 35500589056 | bytes 88088576 | tf_op jit(solution)/shard_map/bnf,fe->bne/dot_general | solution.py:42
  1448.7 0.0 copy-start.1
  1448.7 0.1 all-reduce.7.cloned.1.call-update
  1448.7 177.5 %all-reduce.7.cloned.1.call-done = bf16[32,256,1024]{2,1,0:T(8,128)(2,1)} async-done(((bf16[32,256,1024]{2,1,0:T(8,128)(2,1)}), bf16[32,256,1024]{2,1,0:T(8,128)(2,1)}) %all-reduce.7.cloned.1.call-update) | async-done | bytes 16777232 | tf_op jit(solution)/shard_map/psum | solution.py:43
  1626.2 0.0 copy-done.4
  1626.2 19.9 %fusion.19 = bf16[32,256,1024]{2,1,0:T(8,128)(2,1)} fusion(bf16[32,256,1024]{2,1,0:T(8,128)(2,1)} %param.10, bf16[32,256,1024]{2,1,0:T(8,128)(2,1)} %all-reduce.7.cloned.1.call-done, f32[1024]{0:T(1024)S(1)} %copy-done.4), kind=kLoop, calls=%fused_computation.32 | loop fusion | flops 41943040 | bytes 50335744 | tf_op jit(solution)/shard_map/convert_element_type | solution.py:44
  1646.1 0.0 copy-done.1
Async XLA Ops:
  6.5 48.4 %copy-start = (bf16[1024,3,512]{2,0,1:T(8,128)(2,1)S(1)}, bf16[1024,3,512]{2,0,1:T(8,128)(2,1)}, u32[]{:S(2)}) copy-start(bf16[1024,3,512]{2,0,1:T(8,128)(2,1)} %param.14) | copy-start | bytes 9437188
  6.6 46.9 %all-reduce.5.cloned.1.call-start = ((), (), s32[]{:S(2)}) async-start(), calls=%async_computation | async-start | bytes 131072 | tf_op jit(solution)/shard_map/psum | solution.py:27
  15.2 1140.5 %all-reduce.9.cloned.1.call-start = ((), (), s32[]{:S(2)}) async-start(), calls=%async_computation.2 | async-start | bytes 117440512 | tf_op jit(solution)/shard_map/psum | solution.py:33
  189.0 996.0 %copy-start.2 = (f32[128]{0:T(128)S(1)}, f32[128]{0:T(128)}, u32[]{:S(2)}) copy-start(f32[128]{0:T(128)} %param.13) | copy-start | bytes 1540
  189.0 996.0 %copy-start.3 = (f32[128]{0:T(128)S(1)}, f32[128]{0:T(128)}, u32[]{:S(2)}) copy-start(f32[128]{0:T(128)} %param.12) | copy-start | bytes 1540
  189.1 1437.1 %all-reduce.7.cloned.1.call-start = ((), (), s32[]{:S(2)}) async-start(), calls=%async_computation.1 | async-start | bytes 33554432 | tf_op jit(solution)/shard_map/psum | solution.py:43
  1208.6 34.9 %copy-start.5 = (bf16[512,1024]{1,0:T(8,128)(2,1)S(1)}, bf16[512,1024]{1,0:T(8,128)(2,1)}, u32[]{:S(2)}) copy-start(bf16[512,1024]{1,0:T(8,128)(2,1)} %param.17) | copy-start | bytes 3145732
  1243.5 28.0 %copy-start.6 = (f32[2048]{0:T(1024)S(1)}, f32[2048]{0:T(1024)}, u32[]{:S(2)}) copy-start(f32[2048]{0:T(1024)} %param.16) | copy-start | bytes 24580
  1271.4 354.8 %copy-start.4 = (f32[1024]{0:T(1024)S(1)}, f32[1024]{0:T(1024)}, u32[]{:S(2)}) copy-start(f32[1024]{0:T(1024)} %param.19) | copy-start | bytes 12292
  1448.7 197.5 %copy-start.1 = (bf16[1024,3,512]{2,0,1:T(8,128)(2,1)S(1)}, bf16[1024,3,512]{2,0,1:T(8,128)(2,1)}, u32[]{:S(2)}) copy-start(bf16[1024,3,512]{2,0,1:T(8,128)(2,1)} %param.14) | copy-start | bytes 9437188
Sparse Core Ops, SparseCore 0:
  15.4 38.0 all-reduce.4
  189.2 966.4 all-reduce.8
  1448.8 177.3 all-reduce.6
where the time goes:
time: 1660 us; the launch traced here: 1650 us
  waiting for transfers between devices  1180 us (71%)
  matrix products  305 us (18%)
  other arithmetic  94.1 us (6%)
  local copies, waits for them, and re-layouts  58.1 us (4%)
    psum x1, waiting for transfers between devices, local_layer(): proj_qkv, up_in = lax.psum((qkv_part, up_part), 'm1')  967 us
    psum x1, waiting for transfers between devices, local_layer(): mixed_sum = lax.psum(out_part.astype(jnp.bfloat16), 'm2')  178 us
    dot_general x1, matrix products, local_layer(): jnp.einsum('bnf,fe->bne', hidden, w_down, preferred_element_type=jnp.floa...  177 us
    reshape x2, local copies, waits for them, and re-layouts, local_layer(): proj_qkv = proj_qkv.reshape(batch, patches, 3, heads_local, head_dim)  57.4 us
    dot_general x1, matrix products, local_layer(): jnp.einsum('bnd,df->bnf', normed, w_up, preferred_element_type=jnp.float32)  43.5 us
    psum x1, waiting for transfers between devices, local_layer(): moments = lax.psum(moments, 'm1')  37.4 us
    sub x1, other arithmetic, local_layer(): attn_probs = jax.nn.softmax(scores, axis=-1).astype(jnp.bfloat16)  34.9 us
  transfers between devices with their start and end apart: 3, of which 3 were waited for; matrix products, arithmetic and copies ran while one was open for 0% of the time, Pallas kernels for 0%

commit v1 on v0

v1 whole, which is shorter than its diff:
```python
import functools

import jax
import jax.numpy as jnp
from jax import lax
from jax.experimental import pallas as pl
from jax.experimental.pallas import tpu as pltpu
from jax.sharding import PartitionSpec as P

LN_EPS = 1e-6
CORES = 2
LINES = 16
VMEM_MAX = 67043328
MESH = pl.DeviceIdType.MESH


def layer_norm(values, scale):
    mean = jnp.mean(values, axis=-1, keepdims=True)
    centered = values - mean
    variance = jnp.mean(centered * centered, axis=-1, keepdims=True)
    return centered * lax.rsqrt(variance + LN_EPS) * scale


class Place:
    def __init__(self, rows, chips):
        self.rows, self.chips = rows, chips
        self.dp, self.row = lax.axis_index('dp'), lax.axis_index('m1')
        col = lax.axis_index('m2')
        self.col, self.chip, self.core = col, col // CORES, lax.rem(col, CORES)
        self.inner = self.row + 1 - 2 * lax.rem(self.row, 2)
        self.cross = rows - 1 - self.row
        self.pair = self.row // 2
        self.half = lax.rem((self.row + 1) // 2, 2)
        self.primary = self.core == self.pair
        self.inner_peer = (self.dp, self.inner, col)
        self.cross_peer = (self.dp, self.cross, col)
        self.right_peer = (self.dp, self.row, self.at(1) * CORES + self.core)
        self.left_peer = (self.dp, self.row, self.at(chips - 1) * CORES + self.core)
        self.sibling = (self.dp, self.row, self.chip * CORES + 1 - self.core)

    def at(self, dx):
        return lax.rem(self.chip + dx, self.chips)

    def enter(self):
        barrier = pltpu.get_barrier_semaphore()
        partners = (self.inner_peer, self.cross_peer, self.right_peer, self.left_peer, self.sibling)
        for who in partners:
            pl.semaphore_signal(barrier, inc=1, device_id=who, device_id_type=MESH)
        pl.semaphore_wait(barrier, len(partners))

    def first_image(self, half, dx, core, batch):
        per = batch // (2 * CORES)
        return (half * CORES + core) * per + self.at(dx) * (per // self.chips)


def remote(src, dst, ssem, rsem, who):
    return pltpu.make_async_remote_copy(src_ref=src, dst_ref=dst, send_sem=ssem, recv_sem=rsem, device_id=who, device_id_type=MESH)


def aligned(index, size):
    return pl.ds(pl.multiple_of(index * size, size), size)


def stage_one_kernel(rows, chips, heads, x_hbm, ln_scale, qk_scale, bias_own, wq, wu, h_hbm, raw, u_v, w_v, qkv_v, st_v, up_v, at_v, bias_v,
                     xs_send, xs_recv, ag_send, ag_recv, ld_sem, own_sem, b_send, b_recv, wa_send, wa_recv, wb_send, wb_recv, wc_send, wc_recv,
                     wd_send, wd_recv, up_sem, at_sem):
    p = Place(rows, chips)
    batch, patches, dim_local = x_hbm.shape
    dim = dim_local * rows
    wide = wq.shape[2]
    head_dim = wide // heads
    n_q, n_up = wq.shape[0], wu.shape[1] // wide
    n_w = n_q + n_up
    sub = batch // (2 * CORES * chips)
    group = sub * patches
    dx_of = (0, chips - 1, 1, 2)

    xa = remote(x_hbm.at[pl.ds(p.first_image(p.half, 0, p.core, batch), sub)], raw.at[0, 1], xs_send.at[0], xs_recv.at[0], p.cross_peer)
    xb = remote(x_hbm.at[pl.ds(p.first_image(1 - p.half, 0, p.core, batch), sub)], raw.at[0, 0], xs_send.at[1], xs_recv.at[1], p.inner_peer)
    xc = remote(raw.at[0, 0], raw.at[0, 2], xs_send.at[2], xs_recv.at[2], p.cross_peer)

    def ag(e, k):
        src, dst = ((raw.at[0, e], raw.at[1, e]), (raw.at[0, e], raw.at[2, e]), (raw.at[1, e, 0], raw.at[3, e, 0]), (raw.at[2, e, 1], raw.at[3, e, 1]))[k]
        return remote(src, dst, ag_send.at[e, k], ag_recv.at[e, k], p.right_peer if k % 2 == 0 else p.left_peer)

    def block(r, k):
        return w_v.at[pl.ds(r * dim_local, dim_local), aligned(k, wide)]

    def from_own(k, make, act):
        @pl.when(k < n_q)
        def _():
            act(make(wq.at[jnp.minimum(k, n_q - 1)]))

        @pl.when(k >= n_q)
        def _():
            act(make(wu.at[:, aligned(jnp.maximum(k - n_q, 0), wide)]))

    def wa(k, src=None):
        return remote(block(1, k) if src is None else src, block(1, k), wa_send.at[k], wa_recv.at[k], p.inner_peer)

    def wb(k, src=None):
        return remote(block(2, k) if src is None else src, block(2, k), wb_send.at[k], wb_recv.at[k], p.cross_peer)

    def wc(k):
        return remote(block(2, k), block(3, k), wc_send.at[k], wc_recv.at[k], p.inner_peer)

    def wd(r, k, src=None):
        return remote(block(r, k) if src is None else src, block(r, k), wd_send.at[r, k], wd_recv.at[r, k], p.sibling)

    own_copies = [pltpu.make_async_copy(wq.at[k], block(0, k), own_sem.at[k]) for k in range(n_q)]
    own_copies.append(pltpu.make_async_copy(wu, w_v.at[pl.ds(0, dim_local), pl.ds(n_q * wide, n_up * wide)], own_sem.at[n_q]))
    bias_copy = remote(bias_own, bias_v, b_send, b_recv, p.sibling)

    def start(copy):
        copy.start()

    def pump(k):
        @pl.when(p.primary)
        def _():
            wb(k).wait_recv()
            wc(k).start()
            wd(2, k).start()
            wa(k).wait_recv()
            wd(1, k).start()
            if k + 2 < n_w:
                from_own(k + 2, functools.partial(wa, k + 2), start)
                from_own(k + 2, functools.partial(wd, 0, k + 2), start)

    def finish(k):
        @pl.when(p.primary)
        def _():
            wc(k).wait_recv()
            wd(3, k).start()

        @pl.when(jnp.logical_not(p.primary))
        def _():
            for r in range(rows):
                wd(r, k).wait_recv()

    def load_copies(rank_dx, rank, s, b):
        image = p.first_image(p.half, rank_dx, p.core, batch) + s
        yield pltpu.make_async_copy(x_hbm.at[image], st_v.at[b, :, pl.ds(0, dim_local)], ld_sem.at[b, 0])
        for e in range(rows - 1):
            yield pltpu.make_async_copy(raw.at[rank, e, s], st_v.at[b, :, pl.ds((e + 1) * dim_local, dim_local)], ld_sem.at[b, e + 1])

    def normalize(ranks):
        jobs = [(rank, s) for rank in ranks for s in range(sub)]
        loads = [list(load_copies(dx_of[rank], rank, s, n % 2)) for n, (rank, s) in enumerate(jobs)]
        for n in range(len(jobs)):
            if n == 0:
                for c in loads[0]:
                    c.start()
            if n + 1 < len(jobs):
                for c in loads[n + 1]:
                    c.start()
            for c in loads[n]:
                c.wait()
            rank, s = jobs[n]

            def lines(m, carry, b=n % 2, base=(rank * sub + s) * patches):
                here = aligned(m, LINES)
                wide_x = st_v[b, here, :].astype(jnp.float32)
                to = pl.ds(pl.multiple_of(base + m * LINES, LINES), LINES)
                u_v[to, :] = layer_norm(wide_x, ln_scale[...]).astype(jnp.bfloat16)
                return carry

            lax.fori_loop(0, patches // LINES, lines, 0)

    def dot_cell(rank, k):
        return jnp.dot(u_v[aligned(rank, group), :], w_v[:, aligned(k, wide)], preferred_element_type=jnp.float32).astype(jnp.bfloat16)

    def qkv_cell(rank, k):
        z = dot_cell(rank, k)
        to = aligned(rank, group)

        @pl.when(k == n_q - 1)
        def _():
            qkv_v[k, to, :] = z

        @pl.when(k < n_q - 1)
        def _():
            scale = qk_scale[pl.ds(k, 1), :]
            for hd in range(heads):
                part = slice(hd * head_dim, (hd + 1) * head_dim)
                qkv_v[k, to, part] = layer_norm(z[:, part].astype(jnp.float32), scale).astype(jnp.bfloat16)

    def at_copy(image, b):
        return pltpu.make_async_copy(at_v.at[b], h_hbm.at[aligned(image, patches), pl.ds(0, wide)], at_sem.at[b])

    def attend(first, count):
        def one(image, carry):
            b = lax.rem(image, 2)
            here = aligned(image, patches)

            @pl.when(image >= 2)
            def _():
                at_copy(image - 2, b).wait()

            for hd in range(heads):
                part = slice(hd * head_dim, (hd + 1) * head_dim)
                q, k, v = (qkv_v[n, here, part] for n in range(3))
                scores = lax.dot_general(q, k, (((1,), (1,)), ((), ())), preferred_element_type=jnp.float32) * head_dim ** -0.5
                probs = jnp.exp(scores - jnp.max(scores, axis=-1, keepdims=True))
                probs = (probs / jnp.sum(probs, axis=-1, keepdims=True)).astype(jnp.bfloat16)
                at_v[b, :, part] = jnp.dot(probs, v, preferred_element_type=jnp.float32).astype(jnp.bfloat16)
            at_copy(image, b).start()
            return carry

        lax.fori_loop(first, first + count, one, 0)

    def up_copy(rank, k, b):
        return pltpu.make_async_copy(up_v.at[b], h_hbm.at[aligned(rank, group), aligned(k - n_q + 1, wide)], up_sem.at[b])

    def up_chunk(k, carry):
        finish(k)
        here = aligned(k - n_q, wide)
        bias = jnp.where(p.primary, bias_own[:, here], bias_v[:, here])

        def cell(rank, carry):
            b = lax.rem(rank, 2)

            @pl.when(jnp.logical_or(k > n_q, rank >= 2))
            def _():
                up_copy(rank, k, b).wait()

            m = dot_cell(rank, k).astype(jnp.float32) + bias
            up_v[b] = (0.5 * m * (1.0 + lax.erf(m * 0.5 ** 0.5))).astype(jnp.bfloat16)
            up_copy(rank, k, b).start()
            return carry

        return lax.fori_loop(0, rows, cell, carry)

    p.enter()
    xb.start()
    xa.start()
    bias_copy.start()

    @pl.when(p.primary)
    def _():
        for c in own_copies:
            c.start()
        for k in (0, 1):
            from_own(k, functools.partial(wa, k), start)
            from_own(k, functools.partial(wd, 0, k), start)

    @pl.when(jnp.logical_not(p.primary))
    def _():
        from_own(0, functools.partial(wb, 0), start)

    xb.wait_recv()
    xc.start()
    ag(0, 0).start()
    ag(0, 1).start()

    @pl.when(jnp.logical_not(p.primary))
    def _():
        for k in range(1, n_w):
            from_own(k, functools.partial(wb, k), start)

    xa.wait_recv()
    ag(1, 0).start()
    ag(1, 1).start()
    pump(0)
    xc.wait_recv()
    ag(2, 0).start()
    ag(2, 1).start()
    pump(1)
    normalize((0,))
    for e in range(rows - 1):
        for k in range(2):
            ag(e, k).wait_recv()
            ag(e, 2 + k).start()
        if e == 0:
            pump(2)
    pump(3)
    normalize((1, 2))

    @pl.when(p.primary)
    def _():
        for c in own_copies:
            c.wait()

    def first_ranks(k, carry):
        finish(k)

        @pl.when(k == 1)
        def _():
            pump(4)

        def cell(rank, carry):
            qkv_cell(rank, k)
            return carry

        return lax.fori_loop(0, rows - 1, cell, carry)

    lax.fori_loop(0, n_q, first_ranks, 0)
    attend(0, (rows - 1) * sub)
    pump(5)
    for e in range(rows - 1):
        ag(e, 2).wait_recv()
        ag(e, 3).wait_recv()
    normalize((rows - 1,))

    def last_rank(k, carry):
        qkv_cell(rows - 1, k)
        return carry

    lax.fori_loop(0, n_q, last_rank, 0)
    pump(6)
    attend((rows - 1) * sub, sub)
    bias_copy.wait_recv()
    lax.fori_loop(n_q, n_w, up_chunk, 0)

    for b in range(2):
        at_copy(b, b).wait()
        up_copy(b, n_q, b).wait()
    for c in (xa, xb, xc, bias_copy):
        c.wait_send()
    for e in range(rows - 1):
        for k in range(4):
            ag(e, k).wait_send()

    @pl.when(p.primary)
    def _():
        for k in range(n_w):
            wa(k).wait_send()
            wc(k).wait_send()
            for r in range(rows):
                wd(r, k).wait_send()

    @pl.when(jnp.logical_not(p.primary))
    def _():
        for k in range(n_w):
            wb(k).wait_send()


def stage_one(rows, chips, x_blk, ln_scale, qk_scale, b_up, wq, wu):
    batch, patches, dim_local = x_blk.shape
    dim, wide = rows * dim_local, wq.shape[2]
    heads = wide // qk_scale.shape[1]
    n_q, n_up = wq.shape[0], wu.shape[1] // wide
    n_w = n_q + n_up
    sub = batch // (2 * CORES * chips)
    tokens = chips * sub * patches
    bf, vm, dma = jnp.bfloat16, pltpu.VMEM, pltpu.SemaphoreType.DMA
    anyspec, vmspec = pl.BlockSpec(memory_space=pl.ANY), pl.BlockSpec(memory_space=pltpu.VMEM)
    h, _ = pl.pallas_call(
        functools.partial(stage_one_kernel, rows, chips, heads),
        out_shape=(jax.ShapeDtypeStruct((tokens, wide + n_up * wide), bf), jax.ShapeDtypeStruct((chips, rows - 1, sub, patches, dim_local), bf)),
        in_specs=[anyspec, vmspec, vmspec, vmspec, anyspec, anyspec],
        out_specs=(anyspec, anyspec),
        scratch_shapes=[
            vm((tokens, dim), bf), vm((dim, n_w * wide), bf), vm((n_q, tokens, wide), bf), vm((2, patches, dim), bf),
            vm((2, sub * patches, wide), bf), vm((2, patches, wide), bf), vm(b_up.shape, jnp.float32),
            dma((3,)), dma((3,)), dma((rows - 1, 4)), dma((rows - 1, 4)), dma((2, rows)), dma((n_q + 1,)), dma, dma,
            dma((n_w,)), dma((n_w,)), dma((n_w,)), dma((n_w,)), dma((n_w,)), dma((n_w,)), dma((rows, n_w)), dma((rows, n_w)), dma((2,)), dma((2,)),
        ],
        compiler_params=pltpu.CompilerParams(collective_id=0, has_side_effects=True, vmem_limit_bytes=VMEM_MAX),
        cost_estimate=pl.CostEstimate(flops=2 * tokens * dim * n_w * wide, bytes_accessed=1 << 27, transcendentals=0),
        name='stage_one',
    )(x_blk, ln_scale, qk_scale, b_up, wq, wu)
    return h


def stage_two_kernel(rows, chips, x_hbm, h_hbm, w_o, w_down, bias, out_hbm, h_v, w_v, x_v, rx_v, half_v, tot_v, ry_v, fin_v,
                     ld_sem, wa_send, wa_recv, wb_send, wb_recv, wc_send, wc_recv, wd_send, wd_recv, hf_send, hf_recv, x_send, x_recv,
                     y_send, y_recv, g_send, g_recv, s_send, s_recv, l_sem):
    p = Place(rows, chips)
    batch, patches, dim_local = x_hbm.shape
    sub = batch // (2 * CORES * chips)
    group = sub * patches
    ko = w_o.shape[0]
    kd = w_down.shape[0]
    order = (0, 1, 2, 3)

    def two(slot, send, recv, who):
        return [remote(w_o, w_v.at[slot, pl.ds(0, ko), :], send.at[0], recv.at[0], who), remote(w_down, w_v.at[slot, pl.ds(ko, kd), :], send.at[1], recv.at[1], who)]

    wa = two(1, wa_send, wa_recv, p.inner_peer)
    wb = two(2, wb_send, wb_recv, p.cross_peer)
    wc = remote(w_v.at[2], w_v.at[3], wc_send, wc_recv, p.inner_peer)
    wd0 = two(0, wd_send, wd_recv, p.sibling)
    wd = [None] + [remote(w_v.at[r], w_v.at[r], wd_send.at[r + 1], wd_recv.at[r + 1], p.sibling) for r in (1, 2, 3)]
    own = [pltpu.make_async_copy(w_o, w_v.at[0, pl.ds(0, ko), :], ld_sem.at[0]), pltpu.make_async_copy(w_down, w_v.at[0, pl.ds(ko, kd), :], ld_sem.at[1])]
    h_copy = pltpu.make_async_copy(h_hbm, h_v, ld_sem.at[2])

    def images(side, dx, core=None):
        half = p.half if side == 0 else 1 - p.half
        return p.first_image(half, dx, p.core if core is None else core, batch)

    fin_load = [pltpu.make_async_copy(x_hbm.at[pl.ds(images(side, 0), sub)], fin_v.at[side], ld_sem.at[3 + side]) for side in (0, 1)]

    def half_copy(q, k):
        who = p.right_peer if k == 0 else p.left_peer
        return remote(x_v.at[q % 2, 3, k], half_v.at[q % 2, k], hf_send.at[q, k], hf_recv.at[q, k], who)

    def x_copy(q, k):
        who = p.right_peer if k == 0 else p.left_peer
        return remote(x_v.at[q % 2, 2 - k], rx_v.at[q % 2, k], x_send.at[q, k], x_recv.at[q, k], who)

    def y_copy(n):
        src, who = ((2, p.cross_peer), (3, p.cross_peer), (1, p.inner_peer))[n]
        return remote(tot_v.at[src], ry_v.at[n], y_send.at[n], y_recv.at[n], who)

    def g_copy(side, k):
        who = p.right_peer if k % 2 == 0 else p.left_peer
        if k < 2:
            src, dst = fin_v.at[side], out_hbm.at[pl.ds(images(side, 0), sub)]
        else:
            image = images(side, chips - 1 if k == 2 else 1) + (k - 2)
            src = dst = out_hbm.at[image]
        return remote(src, dst, g_send.at[side, k], g_recv.at[side, k], who)

    def s_copy(side, k):
        here = out_hbm.at[pl.ds(images(side, (0, chips - 1, 1, 2)[k]), sub)]
        return remote(fin_v.at[side] if k == 0 else here, here, s_send.at[side, k], s_recv.at[side, k], p.sibling)

    def l_copy(side):
        return pltpu.make_async_copy(fin_v.at[side], out_hbm.at[pl.ds(images(side, 0), sub)], l_sem.at[side])

    def compute(q, r):
        s = q % 2
        if q >= 2:
            for k in range(2):
                half_copy(q - 2, k).wait_send()
                x_copy(q - 2, k).wait_send()

        def cell(n, carry):
            rank = lax.rem(n + 3, chips)
            part = jnp.dot(h_v[aligned(rank, group), :], w_v[r], preferred_element_type=jnp.float32).astype(jnp.bfloat16)
            x_v[s, rank] = part.reshape(sub, patches, dim_local)

            @pl.when(n == 0)
            def _():
                half_copy(q, 0).start()
                half_copy(q, 1).start()

            return carry

        lax.fori_loop(0, chips, cell, 0)

    def add(a, b):
        return a.astype(jnp.float32) + b.astype(jnp.float32)

    def mid(q):
        s = q % 2
        half_copy(q, 0).wait_recv()
        half_copy(q, 1).wait_recv()
        for k in range(2):
            x_v[s, 2 - k, k] = add(x_v[s, 2 - k, k], half_v[s, k]).astype(jnp.bfloat16)
            x_copy(q, k).start()

    def reduce(q, r):
        s = q % 2
        x_copy(q, 0).wait_recv()
        x_copy(q, 1).wait_recv()
        for n in range(sub):
            tot_v[r, n] = (add(x_v[s, 0, n], rx_v[s, 0, n]) + rx_v[s, 1, n].astype(jnp.float32)).astype(jnp.bfloat16)
        if r >= 2:
            y_copy(r - 2).start()

    def pass_on():
        y_copy(1).wait_recv()
        for n in range(sub):
            tot_v[1, n] = add(tot_v[1, n], ry_v[1, n]).astype(jnp.bfloat16)
        y_copy(2).start()

    def home(side):
        y_copy(2 if side else 0).wait_recv()
        fin_load[side].wait()
        for n in range(sub):
            total = ry_v[2, n].astype(jnp.float32) if side else add(tot_v[0, n], ry_v[0, n])
            fin_v[side, n] = (fin_v[side, n].astype(jnp.float32) + total + bias[...]).astype(jnp.bfloat16)
        g_copy(side, 0).start()
        g_copy(side, 1).start()
        s_copy(side, 0).start()
        l_copy(side).start()

    def near(side):
        for k in range(2):
            g_copy(side, k).wait_recv()
            g_copy(side, 2 + k).start()
            s_copy(side, 1 + k).start()

    def far(side):
        g_copy(side, 2).wait_recv()
        g_copy(side, 3).wait_recv()
        s_copy(side, 3).start()

    p.enter()

    @pl.when(p.primary)
    def _():
        for c in wa + own + wd0:
            c.start()

    @pl.when(jnp.logical_not(p.primary))
    def _():
        for c in wb:
            c.start()

    h_copy.start()
    for c in fin_load:
        c.start()
    h_copy.wait()

    @pl.when(p.primary)
    def _():
        for c in own:
            c.wait()

    @pl.when(jnp.logical_not(p.primary))
    def _():
        for c in wd0:
            c.wait_recv()

    compute(0, 0)
    mid(0)
    reduce(0, 0)

    @pl.when(p.primary)
    def _():
        for c in wb:
            c.wait_recv()
        wc.start()
        wd[2].start()
        for c in wa:
            c.wait_recv()
        wd[1].start()

    @pl.when(jnp.logical_not(p.primary))
    def _():
        wd[1].wait_recv()

    compute(1, 1)
    mid(1)

    @pl.when(jnp.logical_not(p.primary))
    def _():
        wd[2].wait_recv()

    compute(2, 2)
    mid(2)
    reduce(1, 1)
    reduce(2, 2)

    @pl.when(p.primary)
    def _():
        wc.wait_recv()
        wd[3].start()

    @pl.when(jnp.logical_not(p.primary))
    def _():
        wd[3].wait_recv()

    compute(3, 3)
    mid(3)
    home(0)
    reduce(3, 3)
    near(0)
    pass_on()
    far(0)
    home(1)
    near(1)
    far(1)

    for side in (0, 1):
        for k in range(4):
            s_copy(side, k).wait_recv()
            s_copy(side, k).wait_send()
            g_copy(side, k).wait_send()
        l_copy(side).wait()
    for n in range(3):
        y_copy(n).wait_send()
    for q in (2, 3):
        for k in range(2):
            half_copy(q, k).wait_send()
            x_copy(q, k).wait_send()

    @pl.when(p.primary)
    def _():
        for c in wa + wd0 + [wc] + wd[1:]:
            c.wait_send()

    @pl.when(jnp.logical_not(p.primary))
    def _():
        for c in wb:
            c.wait_send()


def stage_two(rows, chips, x_blk, h, w_o, w_down, b_out):
    batch, patches, dim_local = x_blk.shape
    sub = batch // (2 * CORES * chips)
    k_dim = w_o.shape[0] + w_down.shape[0]
    bf, vm, dma = jnp.bfloat16, pltpu.VMEM, pltpu.SemaphoreType.DMA
    piece = (sub, patches, dim_local)
    anyspec, vmspec = pl.BlockSpec(memory_space=pl.ANY), pl.BlockSpec(memory_space=pltpu.VMEM)
    return pl.pallas_call(
        functools.partial(stage_two_kernel, rows, chips),
        out_shape=jax.ShapeDtypeStruct(x_blk.shape, bf),
        in_specs=[anyspec] * 4 + [vmspec],
        out_specs=anyspec,
        scratch_shapes=[
            vm(h.shape, bf), vm((rows, k_dim, dim_local), bf), vm((2, chips) + piece, bf), vm((2, 2) + piece, bf), vm((2, 2, patches, dim_local), bf),
            vm((rows,) + piece, bf), vm((3,) + piece, bf), vm((2,) + piece, bf),
            dma((5,)), dma((2,)), dma((2,)), dma((2,)), dma((2,)), dma, dma, dma((5,)), dma((5,)), dma((rows, 2)), dma((rows, 2)), dma((rows, 2)), dma((rows, 2)),
            dma((3,)), dma((3,)), dma((2, 4)), dma((2, 4)), dma((2, 4)), dma((2, 4)), dma((2,)),
        ],
        compiler_params=pltpu.CompilerParams(collective_id=1, has_side_effects=True, vmem_limit_bytes=VMEM_MAX),
        cost_estimate=pl.CostEstimate(flops=2 * h.shape[0] * k_dim * dim_local * rows, bytes_accessed=1 << 27, transcendentals=0),
        name='stage_two',
    )(x_blk, h, w_o, w_down, b_out.reshape(1, dim_local))


def solution(mesh):
    rows, cols = mesh.shape['m1'], mesh.shape['m2']
    chips = cols // CORES
    assert rows == 4 and chips == 4

    def local_layer(x_blk, ln_scale, qn_scale, kn_scale, w_qkv, w_up, b_up, w_o, w_down, b_out):
        dim_local = x_blk.shape[2]
        row = lax.axis_index('m1')
        inner, cross = row + 1 - 2 * lax.rem(row, 2), rows - 1 - row
        seen = (row, inner, cross, lax.rem(row + 2, rows))
        scale = jnp.concatenate([lax.dynamic_slice_in_dim(ln_scale, r * dim_local, dim_local) for r in seen])
        h = stage_one(rows, chips, x_blk, scale[None], jnp.stack([qn_scale, kn_scale]), b_up[None], w_qkv.transpose(1, 0, 2), w_up)
        return stage_two(rows, chips, x_blk, h, w_o, w_down, b_out)

    return jax.shard_map(local_layer, mesh=mesh, in_specs=(P('dp', None, 'm1'), P(), P(), P(), P('m1', None, 'm2'), P('m1', 'm2'), P('m2'), P('m2', 'm1'), P('m2', 'm1'), P('m1')), out_specs=P('dp', None, 'm1'), check_vma=False)
```

time: 1660 us -> 499 us (0.30)
  waiting for transfers between devices: 1180 us -> 0 us
  Pallas kernels: 0 us -> 481 us
  matrix products: 305 us -> 0 us
  other arithmetic: 94.1 us -> 1.88 us
  local copies, waits for them, and re-layouts: 58.1 us -> 14.6 us
    psum x3 -> x0, waiting for transfers between devices: 1180 us -> none  [the longest x1 967 us: local_layer(): proj_qkv, up_in = lax.psum((qkv_part, up_part), 'm1')]
    pallas_call x0 -> x2, Pallas kernels: none -> 481 us  [the longest x1 264 us: stage_two(): pl.pallas_call(functools.partial(stage_two_kernel, rows, chips), out_shap...]
    dot_general x5 -> x0, matrix products: 305 us -> none  [the longest x1 177 us: local_layer(): jnp.einsum('bnf,fe->bne', hidden, w_down, preferred_element_type=jnp.floa...]
    reshape x2 -> x0, local copies, waits for them, and re-layouts: 57.4 us -> none  [local_layer(): proj_qkv = proj_qkv.reshape(batch, patches, 3, heads_local, head_dim)]
    reduce_sum x3 -> x0, other arithmetic: 37 us -> none  [the longest x1 20.3 us: layer_norm(): variance = jnp.mean(centered * centered, axis=-1, keepdims=True)]
    sub x1 -> x0, other arithmetic: 34.9 us -> none  [local_layer(): attn_probs = jax.nn.softmax(scores, axis=-1).astype(jnp.bfloat16)]
    convert_element_type x1 -> x0, other arithmetic: 19.9 us -> none  [local_layer(): return (x_wide + mixed_sum.astype(jnp.float32) + b_out).astype(jnp.bfloat16)]
  transfers between devices with their start and end apart: 3 -> 0, of which waited for: 3 -> 0; matrix products, arithmetic and copies ran while one was open for 0% -> 0% of each run, Pallas kernels for 0% -> 0%
where the time goes in v1:
time: 499 us; the launch traced here: 497 us
  Pallas kernels  481 us (96%)
  local copies, waits for them, and re-layouts  14.6 us (3%)
    pallas_call x1, Pallas kernels, stage_two(): pl.pallas_call(functools.partial(stage_two_kernel, rows, chips), out_shap...  264 us
    pallas_call x1, Pallas kernels, stage_one(): pl.pallas_call(functools.partial(stage_one_kernel, rows, chips, heads), o...  216 us
    unnamed x1, local copies, waits for them, and re-layouts  13.9 us

profile of v1, /device:TPU:97, one launch (start us, length us, event | category | flops | bytes accessed | tf_op | source)
XLA Modules:
  0.0 497.5 jit_solution(11252022835834291883)
XLA Ops:
  0.0 1.3 pad_maximum_fusion.1.qk_scale
  1.3 0.7 fusion
  2.0 0.6 pad_maximum_fusion
  2.6 216.4 %stage_one.1 = (bf16[2048,2560]{1,0:T(8,128)(2,1)}, bf16[4,3,2,256,1024]{4,3,2,1,0:T(8,128)(2,1)}) custom-call(bf16[32,256,1024]{2,1,0:T(8,128)(2,1)} %x_hbm.3, f32[1,4096]{1,0:T(1,128)} %bitcast.6, f32[2,128]{1,0:T(2,128)} %pad_maximum_fusion.1.qk_scale, f32[1,2048]{1,0:T(1,128)} %bitcast.10, bf16[3,1024,512]{2,1,0:T(8,128)(2,1)} %bitcast.9, ...), custom_call_target="tpu_custom_call" | custom-call | flops 60129542144 | bytes 134217728 | tf_op jit(solution)/shard_map/stage_one/pallas_call | solution.py:347
  219.1 264.5 %stage_two.1 = bf16[32,256,1024]{2,1,0:T(8,128)(2,1)} custom-call(bf16[32,256,1024]{2,1,0:T(8,128)(2,1)} %x_hbm.3, bf16[2048,2560]{1,0:T(8,128)(2,1)} %get-tuple-element.6.h_hbm, bf16[512,1024]{1,0:T(8,128)(2,1)} %w_o.1, bf16[2048,1024]{1,0:T(8,128)(2,1)} %w_down.1, f32[1,1024]{1,0:T(1,128)} %bitcast.11), custom_call_target="tpu_custom_call" | custom-call | flops 42949672960 | bytes 134217728 | tf_op jit(solution)/shard_map/stage_two/pallas_call | solution.py:598
  483.5 13.9 %copy.12 = bf16[32,256,1024]{2,1,0:T(8,128)(2,1)} copy(bf16[32,256,1024]{2,1,0:T(8,128)(2,1)} %stage_two.1) | data formatting | bytes 33554432

commit v2 on v1

v2 whole, which is shorter than its diff:
```python
import functools

import jax
import jax.numpy as jnp
from jax import lax
from jax.experimental import pallas as pl
from jax.experimental.pallas import tpu as pltpu
from jax.sharding import PartitionSpec as P

LN_EPS = 1e-6
CORES = 2
LINES = 16
LANES = 128
AHEAD = 3
CHUNKS = 2
VMEM_MAX = 67043328
MESH = pl.DeviceIdType.MESH


def layer_norm(values, scale):
    mean = jnp.mean(values, axis=-1, keepdims=True)
    centered = values - mean
    variance = jnp.mean(centered * centered, axis=-1, keepdims=True)
    return centered * lax.rsqrt(variance + LN_EPS) * scale


class Place:
    def __init__(self, rows, chips):
        self.rows, self.chips = rows, chips
        self.dp, self.row = lax.axis_index('dp'), lax.axis_index('m1')
        col = lax.axis_index('m2')
        self.col, self.chip, self.core = col, col // CORES, lax.rem(col, CORES)
        self.inner = self.row + 1 - 2 * lax.rem(self.row, 2)
        self.cross = rows - 1 - self.row
        self.pair = self.row // 2
        self.half = lax.rem((self.row + 1) // 2, 2)
        self.primary = self.core == self.pair
        self.inner_peer = (self.dp, self.inner, col)
        self.cross_peer = (self.dp, self.cross, col)
        self.right_peer = (self.dp, self.row, self.at(1) * CORES + self.core)
        self.left_peer = (self.dp, self.row, self.at(chips - 1) * CORES + self.core)
        self.sibling = (self.dp, self.row, self.chip * CORES + 1 - self.core)

    def at(self, dx):
        return lax.rem(self.chip + dx, self.chips)

    def enter(self):
        barrier = pltpu.get_barrier_semaphore()
        partners = (self.inner_peer, self.cross_peer, self.right_peer, self.left_peer, self.sibling)
        for who in partners:
            pl.semaphore_signal(barrier, inc=1, device_id=who, device_id_type=MESH)
        pl.semaphore_wait(barrier, len(partners))

    def first_image(self, half, dx, core, batch):
        per = batch // (2 * CORES)
        return (half * CORES + core) * per + self.at(dx) * (per // self.chips)


def remote(src, dst, ssem, rsem, who):
    return pltpu.make_async_remote_copy(src_ref=src, dst_ref=dst, send_sem=ssem, recv_sem=rsem, device_id=who, device_id_type=MESH)


def aligned(index, size):
    return pl.ds(pl.multiple_of(index * size, size), size)


def stage_one_kernel(rows, chips, heads, x_hbm, ln_scale, qk_scale, bias_own, wq, wu, w_o, w_down, h_hbm, raw, w2_own, w2_cross, u_v, w_v, qkv_v, st_v, up_v, at_v, bias_v,
                     xs_send, xs_recv, ag_send, ag_recv, ld_sem, own_sem, b_send, b_recv, wa_send, wa_recv, wb_send, wb_recv, wc_send, wc_recv,
                     wd_send, wd_recv, up_sem, at_sem, v_send, v_recv):
    p = Place(rows, chips)
    batch, patches, dim_local = x_hbm.shape
    dim = dim_local * rows
    wide = wq.shape[2]
    head_dim = wide // heads
    n_q, n_up = wq.shape[0], wu.shape[1] // wide
    n_w = n_q + n_up
    sub = batch // (2 * CORES * chips)
    group = sub * patches
    dx_of = (0, chips - 1, 1, 2)

    xa = remote(x_hbm.at[pl.ds(p.first_image(p.half, 0, p.core, batch), sub)], raw.at[0, 1], xs_send.at[0], xs_recv.at[0], p.cross_peer)
    xb = remote(x_hbm.at[pl.ds(p.first_image(1 - p.half, 0, p.core, batch), sub)], raw.at[0, 0], xs_send.at[1], xs_recv.at[1], p.inner_peer)
    xc = remote(raw.at[0, 0], raw.at[0, 2], xs_send.at[2], xs_recv.at[2], p.cross_peer)

    def ag(e, k):
        src, dst = ((raw.at[0, e], raw.at[1, e]), (raw.at[0, e], raw.at[2, e]), (raw.at[1, e, 0], raw.at[3, e, 0]), (raw.at[2, e, 1], raw.at[3, e, 1]))[k]
        return remote(src, dst, ag_send.at[e, k], ag_recv.at[e, k], p.right_peer if k % 2 == 0 else p.left_peer)

    def block(r, k):
        return w_v.at[pl.ds(r * dim_local, dim_local), aligned(k, wide)]

    def from_own(k, make, act):
        @pl.when(k < n_q)
        def _():
            act(make(wq.at[jnp.minimum(k, n_q - 1)]))

        @pl.when(k >= n_q)
        def _():
            act(make(wu.at[:, aligned(jnp.maximum(k - n_q, 0), wide)]))

    def wa(k, src=None):
        return remote(block(1, k) if src is None else src, block(1, k), wa_send.at[k], wa_recv.at[k], p.inner_peer)

    def wb(k, src=None):
        return remote(block(2, k) if src is None else src, block(2, k), wb_send.at[k], wb_recv.at[k], p.cross_peer)

    def wc(k):
        return remote(block(2, k), block(3, k), wc_send.at[k], wc_recv.at[k], p.inner_peer)

    def wd(r, k, src=None):
        return remote(block(r, k) if src is None else src, block(r, k), wd_send.at[r, k], wd_recv.at[r, k], p.sibling)

    own_copies = [pltpu.make_async_copy(wq.at[k], block(0, k), own_sem.at[k]) for k in range(n_q)]
    own_copies.append(pltpu.make_async_copy(wu, w_v.at[pl.ds(0, dim_local), pl.ds(n_q * wide, n_up * wide)], own_sem.at[n_q]))
    bias_copy = remote(bias_own, bias_v, b_send, b_recv, p.sibling)

    ko, kd = w_o.shape[0], w_down.shape[0]

    def two(dst, n, who):
        return [remote(w_o, dst.at[pl.ds(0, ko), :], v_send.at[n], v_recv.at[n], who), remote(w_down, dst.at[pl.ds(ko, kd), :], v_send.at[n + 1], v_recv.at[n + 1], who)]

    v_own, v_cross = two(w2_own, 0, p.sibling), two(w2_cross, 2, p.cross_peer)
    v_pass = remote(w2_cross, w2_cross, v_send.at[4], v_recv.at[4], p.sibling)

    def start(copy):
        copy.start()

    def pump(k):
        @pl.when(p.primary)
        def _():
            wb(k).wait_recv()
            wc(k).start()
            wd(2, k).start()
            wa(k).wait_recv()
            wd(1, k).start()
            if k + AHEAD < n_w:
                from_own(k + AHEAD, functools.partial(wa, k + AHEAD), start)
                from_own(k + AHEAD, functools.partial(wd, 0, k + AHEAD), start)

    def hand_over(k):
        @pl.when(p.primary)
        def _():
            wc(k).wait_recv()
            wd(3, k).start()

    def receive(k):
        @pl.when(jnp.logical_not(p.primary))
        def _():
            for r in range(rows):
                wd(r, k).wait_recv()

    def load_copies(rank_dx, rank, s, b):
        image = p.first_image(p.half, rank_dx, p.core, batch) + s
        yield pltpu.make_async_copy(x_hbm.at[image], st_v.at[b, :, pl.ds(0, dim_local)], ld_sem.at[b, 0])
        for e in range(rows - 1):
            yield pltpu.make_async_copy(raw.at[rank, e, s], st_v.at[b, :, pl.ds((e + 1) * dim_local, dim_local)], ld_sem.at[b, e + 1])

    def normalize(ranks):
        jobs = [(rank, s) for rank in ranks for s in range(sub)]
        loads = [list(load_copies(dx_of[rank], rank, s, n % 2)) for n, (rank, s) in enumerate(jobs)]
        for n in range(len(jobs)):
            if n == 0:
                for c in loads[0]:
                    c.start()
            if n + 1 < len(jobs):
                for c in loads[n + 1]:
                    c.start()
            for c in loads[n]:
                c.wait()
            rank, s = jobs[n]

            def lines(m, carry, b=n % 2, base=(rank * sub + s) * patches):
                here = aligned(m, LINES)
                to = pl.ds(pl.multiple_of(base + m * LINES, LINES), LINES)
                parts = [slice(j * LANES, (j + 1) * LANES) for j in range(dim // LANES)]

                def load(part):
                    return st_v[b, here, part].astype(jnp.float32)

                mean = jnp.sum(functools.reduce(jnp.add, [load(part) for part in parts]), axis=-1, keepdims=True) / dim
                squares = [(load(part) - mean) * (load(part) - mean) for part in parts]
                inverse = lax.rsqrt(jnp.sum(functools.reduce(jnp.add, squares), axis=-1, keepdims=True) / dim + LN_EPS)
                for part in parts:
                    u_v[to, part] = ((load(part) - mean) * inverse * ln_scale[:, part]).astype(jnp.bfloat16)
                return carry

            lax.fori_loop(0, patches // LINES, lines, 0, unroll=4)

    def dot_cell(rank, k):
        return jnp.dot(u_v[aligned(rank, group), :], w_v[:, aligned(k, wide)], preferred_element_type=jnp.float32).astype(jnp.bfloat16)

    def qkv_cell(rank, k):
        z = dot_cell(rank, k)
        to = aligned(rank, group)

        @pl.when(k == n_q - 1)
        def _():
            qkv_v[k, to, :] = z

        @pl.when(k < n_q - 1)
        def _():
            scale = qk_scale[pl.ds(k, 1), :]
            for hd in range(heads):
                part = slice(hd * head_dim, (hd + 1) * head_dim)
                qkv_v[k, to, part] = layer_norm(z[:, part].astype(jnp.float32), scale).astype(jnp.bfloat16)

    def at_copy(image, b):
        return pltpu.make_async_copy(at_v.at[b], h_hbm.at[aligned(image, patches), pl.ds(0, wide)], at_sem.at[b])

    def attend(first, count):
        def one(image, carry):
            b = lax.rem(image, 2)
            here = aligned(image, patches)

            @pl.when(image >= 2)
            def _():
                at_copy(image - 2, b).wait()

            for hd in range(heads):
                part = slice(hd * head_dim, (hd + 1) * head_dim)
                q, k, v = (qkv_v[n, here, part] for n in range(3))
                scores = lax.dot_general(q, k, (((1,), (1,)), ((), ())), preferred_element_type=jnp.float32) * head_dim ** -0.5
                probs = jnp.exp(scores - jnp.max(scores, axis=-1, keepdims=True))
                probs = (probs / jnp.sum(probs, axis=-1, keepdims=True)).astype(jnp.bfloat16)
                at_v[b, :, part] = jnp.dot(probs, v, preferred_element_type=jnp.float32).astype(jnp.bfloat16)
            at_copy(image, b).start()
            return carry

        lax.fori_loop(first, first + count, one, 0)

    def up_copy(rank, k, b):
        return pltpu.make_async_copy(up_v.at[b], h_hbm.at[aligned(rank, group), aligned(k - n_q + 1, wide)], up_sem.at[b])

    def up_chunk(k, carry):
        hand_over(k)
        receive(k)

        @pl.when(jnp.logical_and(p.primary, k == n_w - 1))
        def _():
            for c in v_cross:
                c.wait_recv()
            v_pass.start()

        here = aligned(k - n_q, wide)
        bias = jnp.where(p.primary, bias_own[:, here], bias_v[:, here])

        def cell(rank, carry):
            b = lax.rem(rank, 2)

            @pl.when(jnp.logical_or(k > n_q, rank >= 2))
            def _():
                up_copy(rank, k, b).wait()

            m = dot_cell(rank, k).astype(jnp.float32) + bias
            up_v[b] = (0.5 * m * (1.0 + lax.erf(m * 0.5 ** 0.5))).astype(jnp.bfloat16)
            up_copy(rank, k, b).start()
            return carry

        return lax.fori_loop(0, rows, cell, carry)

    p.enter()
    xb.start()
    xa.start()
    bias_copy.start()

    @pl.when(p.primary)
    def _():
        for c in own_copies:
            c.start()
        for k in range(AHEAD):
            from_own(k, functools.partial(wa, k), start)
            from_own(k, functools.partial(wd, 0, k), start)

    @pl.when(jnp.logical_not(p.primary))
    def _():
        from_own(0, functools.partial(wb, 0), start)

    xb.wait_recv()
    xc.start()
    ag(0, 0).start()
    ag(0, 1).start()

    @pl.when(jnp.logical_not(p.primary))
    def _():
        for k in range(1, n_w):
            from_own(k, functools.partial(wb, k), start)
        for c in v_cross:
            c.start()

    xa.wait_recv()
    ag(1, 0).start()
    ag(1, 1).start()
    pump(0)
    xc.wait_recv()
    ag(2, 0).start()
    ag(2, 1).start()
    normalize((0,))

    def forward(e):
        for k in range(2):
            ag(e, k).wait_recv()
            ag(e, 2 + k).start()

    @pl.when(p.primary)
    def _():
        for c in own_copies:
            c.wait()
        for c in v_own:
            c.start()

    def cells(count, job):
        def cell(n, carry):
            qkv_cell(*job(n))
            return carry

        lax.fori_loop(0, count, cell, 0)

    forward(0)
    hand_over(0)
    pump(1)
    forward(1)
    receive(0)
    cells(1, lambda n: (n, n))
    hand_over(1)
    pump(2)
    receive(1)
    cells(1, lambda n: (n, n + 1))
    forward(2)
    normalize((1, 2))
    hand_over(2)
    pump(3)
    receive(2)
    early = (n_q - 1) * 2
    cells(early + rows - 1, lambda n: (jnp.where(n < early, 1 + lax.rem(n, 2), n - early), jnp.where(n < early, n // 2, n_q - 1)))
    pump(4)
    attend(0, (rows - 1) * sub)
    pump(5)
    for e in range(rows - 1):
        ag(e, 2).wait_recv()
        ag(e, 3).wait_recv()
    normalize((rows - 1,))
    cells(n_q, lambda n: (rows - 1, n))
    pump(6)
    attend((rows - 1) * sub, sub)
    bias_copy.wait_recv()
    lax.fori_loop(n_q, n_w, up_chunk, 0)

    for b in range(2):
        at_copy(b, b).wait()
        up_copy(b, n_q, b).wait()
    for c in (xa, xb, xc, bias_copy):
        c.wait_send()
    for e in range(rows - 1):
        for k in range(4):
            ag(e, k).wait_send()

    @pl.when(p.primary)
    def _():
        for k in range(n_w):
            wa(k).wait_send()
            wc(k).wait_send()
            for r in range(rows):
                wd(r, k).wait_send()
        for c in v_own + [v_pass]:
            c.wait_send()

    @pl.when(jnp.logical_not(p.primary))
    def _():
        for k in range(n_w):
            wb(k).wait_send()
        for c in v_cross:
            c.wait_send()
        for c in v_own + [v_pass]:
            c.wait_recv()


def stage_one(rows, chips, x_blk, ln_scale, qk_scale, b_up, wq, wu, w_o, w_down):
    batch, patches, dim_local = x_blk.shape
    dim, wide = rows * dim_local, wq.shape[2]
    heads = wide // qk_scale.shape[1]
    n_q, n_up = wq.shape[0], wu.shape[1] // wide
    n_w = n_q + n_up
    sub = batch // (2 * CORES * chips)
    tokens = chips * sub * patches
    bf, vm, dma = jnp.bfloat16, pltpu.VMEM, pltpu.SemaphoreType.DMA
    anyspec, vmspec = pl.BlockSpec(memory_space=pl.ANY), pl.BlockSpec(memory_space=pltpu.VMEM)
    w2 = jax.ShapeDtypeStruct((w_o.shape[0] + w_down.shape[0], dim_local), bf)
    h, _, w2_own, w2_cross = pl.pallas_call(
        functools.partial(stage_one_kernel, rows, chips, heads),
        out_shape=(jax.ShapeDtypeStruct((tokens, wide + n_up * wide), bf), jax.ShapeDtypeStruct((chips, rows - 1, sub, patches, dim_local), bf), w2, w2),
        in_specs=[anyspec, vmspec, vmspec, vmspec] + [anyspec] * 4,
        out_specs=(anyspec,) * 4,
        scratch_shapes=[
            vm((tokens, dim), bf), vm((dim, n_w * wide), bf), vm((n_q, tokens, wide), bf), vm((2, patches, dim), bf),
            vm((2, sub * patches, wide), bf), vm((2, patches, wide), bf), vm(b_up.shape, jnp.float32),
            dma((3,)), dma((3,)), dma((rows - 1, 4)), dma((rows - 1, 4)), dma((2, rows)), dma((n_q + 1,)), dma, dma,
            dma((n_w,)), dma((n_w,)), dma((n_w,)), dma((n_w,)), dma((n_w,)), dma((n_w,)), dma((rows, n_w)), dma((rows, n_w)), dma((2,)), dma((2,)), dma((5,)), dma((5,)),
        ],
        compiler_params=pltpu.CompilerParams(collective_id=0, has_side_effects=True, vmem_limit_bytes=VMEM_MAX),
        cost_estimate=pl.CostEstimate(flops=2 * tokens * dim * n_w * wide, bytes_accessed=1 << 27, transcendentals=0),
        name='stage_one',
    )(x_blk, ln_scale, qk_scale, b_up, wq, wu, w_o, w_down)
    return h, w2_own, w2_cross


def stage_two_kernel(rows, chips, x_hbm, h_hbm, w_o, w_down, w2_own, w2_cross, bias, out_hbm, h_v, w_v, ys_v, yt_v, x_v, rx_v, half_v, tot_v, t2_v, in_v, fin_v,
                     ld_sem, wa_send, wa_recv, wc_send, wc_recv, wd_send, wd_recv, hf_send, hf_recv, x_send, x_recv, p_send, p_recv, t_send, t_recv,
                     i_send, i_recv, g_send, g_recv, s_send, s_recv, l_sem):
    p = Place(rows, chips)
    batch, patches, dim_local = x_hbm.shape
    sub = batch // (2 * CORES * chips)
    group = sub * patches
    ko, kd = w_o.shape[0], w_down.shape[0]
    cw = dim_local // CHUNKS
    far_rank = rows - 1

    def cols(c):
        return pl.ds(c * cw, cw)

    def two(c, slot, make):
        return [make(w_o.at[:, cols(c)], w_v.at[c, slot, pl.ds(0, ko), :], 0), make(w_down.at[:, cols(c)], w_v.at[c, slot, pl.ds(ko, kd), :], 1)]

    wa = [two(c, 1, lambda s, d, n, c=c: remote(s, d, wa_send.at[c, n], wa_recv.at[c, n], p.inner_peer)) for c in range(CHUNKS)]
    wc = [remote(w2_cross.at[:, cols(c)], w_v.at[c, 3], wc_send.at[c], wc_recv.at[c], p.inner_peer) for c in range(CHUNKS)]
    wd = [{r: remote(w_v.at[c, r], w_v.at[c, r], wd_send.at[c, r // 2], wd_recv.at[c, r // 2], p.sibling) for r in (1, 3)} for c in range(CHUNKS)]
    own_primary = [two(c, 0, lambda s, d, n, c=c: pltpu.make_async_copy(s, d, ld_sem.at[2 * c + n])) for c in range(CHUNKS)]
    own_other = [pltpu.make_async_copy(w2_own.at[:, cols(c)], w_v.at[c, 0], ld_sem.at[2 * c]) for c in range(CHUNKS)]
    cross_load = [pltpu.make_async_copy(w2_cross.at[:, cols(c)], w_v.at[c, 2], ld_sem.at[2 * CHUNKS + c]) for c in range(CHUNKS)]
    h_copy = pltpu.make_async_copy(h_hbm, h_v, ld_sem.at[3 * CHUNKS])

    def images(side, dx):
        return p.first_image(p.half if side == 0 else 1 - p.half, dx, p.core, batch)

    fin_load = [
        [pltpu.make_async_copy(x_hbm.at[pl.ds(images(side, 0), sub), :, cols(c)], fin_v.at[side, c], ld_sem.at[3 * CHUNKS + 1 + side * CHUNKS + c]) for c in range(CHUNKS)]
        for side in (0, 1)
    ]

    def p_copy(c, rank):
        return remote(ys_v.at[c, rank], yt_v.at[c, rank], p_send.at[c, rank], p_recv.at[c, rank], p.cross_peer)

    def half_copy(u, k):
        who = p.right_peer if k == 0 else p.left_peer
        return remote(x_v.at[u % 3, far_rank, k], half_v.at[u, k], hf_send.at[u, k], hf_recv.at[u, k], who)

    def x_copy(u, k):
        who = p.right_peer if k == 0 else p.left_peer
        return remote(x_v.at[u % 3, 2 - k], rx_v.at[u, k], x_send.at[u, k], x_recv.at[u, k], who)

    def t_copy(c):
        return remote(tot_v.at[1, c], t2_v.at[c], t_send.at[c], t_recv.at[c], p.cross_peer)

    def i_copy(c):
        return remote(tot_v.at[2, c], in_v.at[c], i_send.at[c], i_recv.at[c], p.inner_peer)

    def spot(side, dx, c, count=sub, first=0):
        return out_hbm.at[pl.ds(images(side, dx) + first, count), :, cols(c)]

    def g_copy(side, c, k):
        who = p.right_peer if k % 2 == 0 else p.left_peer
        if k < 2:
            src, dst = fin_v.at[side, c], spot(side, 0, c)
        else:
            src = dst = spot(side, chips - 1 if k == 2 else 1, c, 1, k - 2)
        return remote(src, dst, g_send.at[side, c, k], g_recv.at[side, c, k], who)

    def s_copy(side, c, k):
        here = spot(side, (0, chips - 1, 1, 2)[k], c)
        return remote(fin_v.at[side, c] if k == 0 else here, here, s_send.at[side, c, k], s_recv.at[side, c, k], p.sibling)

    def l_copy(side, c):
        return pltpu.make_async_copy(fin_v.at[side, c], spot(side, 0, c), l_sem.at[side, c])

    def add(a, b):
        return a.astype(jnp.float32) + b.astype(jnp.float32)

    def dot(rank, c, r):
        return jnp.dot(h_v[aligned(rank, group), :], w_v[c, r], preferred_element_type=jnp.float32).astype(jnp.bfloat16).reshape(sub, patches, cw)

    def received(c, r):
        if r in (1, 3):

            @pl.when(jnp.logical_not(p.primary))
            def _():
                wd[c][r].wait_recv()

    def cross_part(c, r):
        received(c, r)

        def cell(n, carry):
            rank = far_rank - n
            ys_v[c, rank] = dot(rank, c, r)
            p_copy(c, rank).start()
            return carry

        lax.fori_loop(0, chips, cell, 0)

    def reuse(u):
        if u >= 3:
            for k in range(2):
                half_copy(u - 3, k).wait_send()
                x_copy(u - 3, k).wait_send()

    def mid_one(u, k):
        half_copy(u, k).wait_recv()
        s = u % 3
        x_v[s, 2 - k, k] = add(x_v[s, 2 - k, k], half_v[u, k]).astype(jnp.bfloat16)
        x_copy(u, k).start()

    def pair_part(u, c, r):
        reuse(u)
        s = u % 3
        received(c, r)

        def cell(n, carry):
            rank = far_rank - n
            part = dot(rank, c, r)
            p_copy(c, rank).wait_recv()
            x_v[s, rank] = add(part, yt_v[c, rank]).astype(jnp.bfloat16)

            @pl.when(n == 0)
            def _():
                half_copy(u, 0).start()
                half_copy(u, 1).start()

            for k in range(2):

                @pl.when(n == k + 1)
                def _(k=k):
                    mid_one(u, k)

            return carry

        lax.fori_loop(0, chips, cell, 0)

    def compute(u, c, r):
        reuse(u)
        s = u % 3
        received(c, r)

        def cell(n, carry):
            rank = far_rank - n
            x_v[s, rank] = dot(rank, c, r)

            @pl.when(n == 0)
            def _():
                half_copy(u, 0).start()
                half_copy(u, 1).start()

            return carry

        lax.fori_loop(0, chips, cell, 0)

    def mid(u):
        mid_one(u, 0)
        mid_one(u, 1)

    def total(u, n):
        s = u % 3
        return add(x_v[s, 0, n], rx_v[u, 0, n]) + rx_v[u, 1, n].astype(jnp.float32)

    def arrived(u):
        x_copy(u, 0).wait_recv()
        x_copy(u, 1).wait_recv()

    def reduce(u, c, slot, send=None):
        arrived(u)
        for n in range(sub):
            tot_v[slot, c, n] = total(u, n).astype(jnp.bfloat16)
        if send is not None:
            send(c).start()

    def fetch_far(c):
        @pl.when(p.primary)
        def _():
            wc[c].wait_recv()
            wd[c][3].start()

    def fetch_inner(c):
        @pl.when(p.primary)
        def _():
            for copy in wa[c]:
                copy.wait_recv()
            wd[c][1].start()

    def pass_on(c):
        t_copy(c).wait_recv()
        for n in range(sub):
            tot_v[2, c, n] = add(tot_v[0, c, n], t2_v[c, n]).astype(jnp.bfloat16)
        i_copy(c).start()

    def home(side, c, u=None):
        if u is None:
            (i_copy if side else t_copy)(c).wait_recv()
        else:
            arrived(u)
        fin_load[side][c].wait()
        for n in range(sub):
            if u is not None:
                summed = total(u, n)
            else:
                summed = in_v[c, n].astype(jnp.float32) if side else add(tot_v[0, c, n], t2_v[c, n])
            fin_v[side, c, n] = (fin_v[side, c, n].astype(jnp.float32) + summed + bias[:, cols(c)]).astype(jnp.bfloat16)
        g_copy(side, c, 0).start()
        g_copy(side, c, 1).start()
        s_copy(side, c, 0).start()
        l_copy(side, c).start()

    def near(side, c):
        for k in range(2):
            g_copy(side, c, k).wait_recv()
            g_copy(side, c, 2 + k).start()
            s_copy(side, c, 1 + k).start()

    def far(side, c):
        g_copy(side, c, 2).wait_recv()
        g_copy(side, c, 3).wait_recv()
        s_copy(side, c, 3).start()

    h_copy.start()
    for c in range(CHUNKS):
        cross_load[c].start()

        @pl.when(p.primary)
        def _(c=c):
            for copy in own_primary[c]:
                copy.start()

        @pl.when(jnp.logical_not(p.primary))
        def _(c=c):
            own_other[c].start()

    for side in (0, 1):
        for c in range(CHUNKS):
            fin_load[side][c].start()
    p.enter()

    @pl.when(p.primary)
    def _():
        for copy in [wc[1], wc[0]] + wa[0] + wa[1]:
            copy.start()

    h_copy.wait()
    for c in range(CHUNKS):

        @pl.when(p.primary)
        def _(c=c):
            for copy in own_primary[c]:
                copy.wait()

        @pl.when(jnp.logical_not(p.primary))
        def _(c=c):
            own_other[c].wait()

        cross_load[c].wait()

    cross_part(0, 2)
    compute(0, 1, 0)
    compute(1, 1, 2)
    mid(0)
    mid(1)
    reduce(0, 1, 0)
    fetch_far(1)
    pair_part(2, 0, 0)
    reduce(1, 1, 1, t_copy)
    cross_part(1, 3)
    fetch_far(0)
    compute(3, 0, 3)
    home(0, 1)
    home(0, 0, 2)
    mid(3)
    near(0, 1)
    near(0, 0)
    reduce(3, 0, 1, t_copy)
    fetch_inner(0)
    compute(4, 0, 1)
    far(0, 1)
    mid(4)
    far(0, 0)
    reduce(4, 0, 0)
    fetch_inner(1)
    pass_on(0)
    pair_part(5, 1, 1)
    home(1, 0)
    reduce(5, 1, 2, i_copy)
    near(1, 0)
    home(1, 1)
    far(1, 0)
    near(1, 1)
    far(1, 1)

    for c in range(CHUNKS):
        for side in (0, 1):
            for k in range(4):
                s_copy(side, c, k).wait_recv()
                s_copy(side, c, k).wait_send()
                g_copy(side, c, k).wait_send()
            l_copy(side, c).wait()
        t_copy(c).wait_send()
        i_copy(c).wait_send()
        for rank in range(chips):
            p_copy(c, rank).wait_send()
    for u in (3, 4, 5):
        for k in range(2):
            half_copy(u, k).wait_send()
            x_copy(u, k).wait_send()

    @pl.when(p.primary)
    def _():
        for c in range(CHUNKS):
            wc[c].wait_send()
            for copy in wa[c]:
                copy.wait_send()
            for r in (1, 3):
                wd[c][r].wait_send()


def stage_two(rows, chips, x_blk, h, w_o, w_down, w2_own, w2_cross, b_out):
    batch, patches, dim_local = x_blk.shape
    sub = batch // (2 * CORES * chips)
    k_dim, cw = w2_own.shape[0], dim_local // CHUNKS
    units = 3 * CHUNKS
    bf, vm, dma = jnp.bfloat16, pltpu.VMEM, pltpu.SemaphoreType.DMA
    piece = (sub, patches, cw)
    anyspec, vmspec = pl.BlockSpec(memory_space=pl.ANY), pl.BlockSpec(memory_space=pltpu.VMEM)
    return pl.pallas_call(
        functools.partial(stage_two_kernel, rows, chips),
        out_shape=jax.ShapeDtypeStruct(x_blk.shape, bf),
        in_specs=[anyspec] * 6 + [vmspec],
        out_specs=anyspec,
        scratch_shapes=[
            vm(h.shape, bf), vm((CHUNKS, rows, k_dim, cw), bf), vm((CHUNKS, chips) + piece, bf), vm((CHUNKS, chips) + piece, bf), vm((3, chips) + piece, bf),
            vm((units, 2) + piece, bf), vm((units, 2, patches, cw), bf), vm((3, CHUNKS) + piece, bf), vm((CHUNKS,) + piece, bf), vm((CHUNKS,) + piece, bf),
            vm((2, CHUNKS) + piece, bf),
            dma((5 * CHUNKS + 1,)), dma((CHUNKS, 2)), dma((CHUNKS, 2)), dma((CHUNKS,)), dma((CHUNKS,)), dma((CHUNKS, 2)), dma((CHUNKS, 2)),
            dma((units, 2)), dma((units, 2)), dma((units, 2)), dma((units, 2)), dma((CHUNKS, chips)), dma((CHUNKS, chips)), dma((CHUNKS,)), dma((CHUNKS,)),
            dma((CHUNKS,)), dma((CHUNKS,)), dma((2, CHUNKS, 4)), dma((2, CHUNKS, 4)), dma((2, CHUNKS, 4)), dma((2, CHUNKS, 4)), dma((2, CHUNKS)),
        ],
        compiler_params=pltpu.CompilerParams(collective_id=1, has_side_effects=True, vmem_limit_bytes=VMEM_MAX),
        cost_estimate=pl.CostEstimate(flops=2 * h.shape[0] * k_dim * dim_local * rows, bytes_accessed=1 << 27, transcendentals=0),
        name='stage_two',
    )(x_blk, h, w_o, w_down, w2_own, w2_cross, b_out.reshape(1, dim_local))


def solution(mesh):
    rows, cols = mesh.shape['m1'], mesh.shape['m2']
    chips = cols // CORES
    assert rows == 4 and chips == 4

    def local_layer(x_blk, ln_scale, qn_scale, kn_scale, w_qkv, w_up, b_up, w_o, w_down, b_out):
        dim_local = x_blk.shape[2]
        row = lax.axis_index('m1')
        inner, cross = row + 1 - 2 * lax.rem(row, 2), rows - 1 - row
        seen = (row, inner, cross, lax.rem(row + 2, rows))
        scale = jnp.concatenate([lax.dynamic_slice_in_dim(ln_scale, r * dim_local, dim_local) for r in seen])
        h, w2_own, w2_cross = stage_one(rows, chips, x_blk, scale[None], jnp.stack([qn_scale, kn_scale]), b_up[None], w_qkv.transpose(1, 0, 2), w_up, w_o, w_down)
        return stage_two(rows, chips, x_blk, h, w_o, w_down, w2_own, w2_cross, b_out)

    return jax.shard_map(local_layer, mesh=mesh, in_specs=(P('dp', None, 'm1'), P(), P(), P(), P('m1', None, 'm2'), P('m1', 'm2'), P('m2'), P('m2', 'm1'), P('m2', 'm1'), P('m1')), out_specs=P('dp', None, 'm1'), check_vma=False)
```

time: 499 us -> 427 us (0.86)
  Pallas kernels: 481 us -> 410 us
    pallas_call x1, Pallas kernels: 264 us -> 203 us  [stage_two(): pl.pallas_call(functools.partial(stage_two_kernel, rows, chips), out_shap...]
    pallas_call x1, Pallas kernels: 216 us -> 207 us  [stage_one(): pl.pallas_call(functools.partial(stage_one_kernel, rows, chips, heads), o...]
where the time goes in v2:
time: 427 us; the launch traced here: 426 us
  Pallas kernels  410 us (96%)
  local copies, waits for them, and re-layouts  14.6 us (3%)
    pallas_call x1, Pallas kernels, stage_one(): pl.pallas_call(functools.partial(stage_one_kernel, rows, chips, heads), o...  207 us
    pallas_call x1, Pallas kernels, stage_two(): pl.pallas_call(functools.partial(stage_two_kernel, rows, chips), out_shap...  203 us
    unnamed x1, local copies, waits for them, and re-layouts  13.9 us

profile of v2, /device:TPU:97, one launch (start us, length us, event | category | flops | bytes accessed | tf_op | source)
XLA Modules:
  0.0 426.4 jit_solution(17718548460910894036)
XLA Ops:
  0.0 1.3 pad_maximum_fusion.1.qk_scale
  1.3 0.7 fusion
  2.0 0.6 pad_maximum_fusion
  2.6 207.0 %stage_one.1 = (bf16[2048,2560]{1,0:T(8,128)(2,1)}, bf16[4,3,2,256,1024]{4,3,2,1,0:T(8,128)(2,1)}, bf16[2560,1024]{1,0:T(8,128)(2,1)}, bf16[2560,1024]{1,0:T(8,128)(2,1)}) custom-call(bf16[32,256,1024]{2,1,0:T(8,128)(2,1)} %x_hbm.3, f32[1,4096]{1,0:T(1,128)} %bitcast.6, f32[2,128]{1,0:T(2,128)} %pad_maximum_fusion.1.qk_scale, f32[1,2048]{1,0:T(1,128)} %bitcast.10, ...), custom_call_target="tpu_custom_call" | custom-call | flops 60129542144 | bytes 134217728 | tf_op jit(solution)/shard_map/stage_one/pallas_call | solution.py:388
  209.7 202.8 %stage_two.1 = bf16[32,256,1024]{2,1,0:T(8,128)(2,1)} custom-call(bf16[32,256,1024]{2,1,0:T(8,128)(2,1)} %x_hbm.3, bf16[2048,2560]{1,0:T(8,128)(2,1)} %get-tuple-element.8.h_hbm, bf16[512,1024]{1,0:T(8,128)(2,1)} %w_o.3, bf16[2048,1024]{1,0:T(8,128)(2,1)} %w_down.3, bf16[2560,1024]{1,0:T(8,128)(2,1)} %get-tuple-element.9.w2_own, ...), custom_call_target="tpu_custom_call" | custom-call | flops 42949672960 | bytes 134217728 | tf_op jit(solution)/shard_map/stage_two/pallas_call | solution.py:726
  412.5 13.9 %copy.12 = bf16[32,256,1024]{2,1,0:T(8,128)(2,1)} copy(bf16[32,256,1024]{2,1,0:T(8,128)(2,1)} %stage_two.1) | data formatting | bytes 33554432

commit v3 on v2

--- a/solution.py
+++ b/solution.py
@@ -11,7 +11,7 @@
 CORES = 2
 LINES = 16
 LANES = 128
-AHEAD = 3
+AHEAD = 2
 CHUNKS = 2
 VMEM_MAX = 67043328
 MESH = pl.DeviceIdType.MESH
@@ -64,9 +64,9 @@
     return pl.ds(pl.multiple_of(index * size, size), size)
 
 
-def stage_one_kernel(rows, chips, heads, x_hbm, ln_scale, qk_scale, bias_own, wq, wu, w_o, w_down, h_hbm, raw, w2_own, w2_cross, u_v, w_v, qkv_v, st_v, up_v, at_v, bias_v,
+def stage_one_kernel(rows, chips, heads, x_hbm, ln_all, qn_scale, kn_scale, bias_own, wq, wu, w_o, w_down, h_hbm, raw, w2_own, w2_cross, u_v, w_v, qkv_v, st_v, up_v, last_v, at_v, bias_v, ln_scale,
                      xs_send, xs_recv, ag_send, ag_recv, ld_sem, own_sem, b_send, b_recv, wa_send, wa_recv, wb_send, wb_recv, wc_send, wc_recv,
-                     wd_send, wd_recv, up_sem, at_sem, v_send, v_recv):
+                     wd_send, wd_recv, up_sem, at_sem, v_send, v_recv, last_sem):
     p = Place(rows, chips)
     batch, patches, dim_local = x_hbm.shape
     dim = dim_local * rows
@@ -120,7 +120,9 @@
         return [remote(w_o, dst.at[pl.ds(0, ko), :], v_send.at[n], v_recv.at[n], who), remote(w_down, dst.at[pl.ds(ko, kd), :], v_send.at[n + 1], v_recv.at[n + 1], who)]
 
     v_own, v_cross = two(w2_own, 0, p.sibling), two(w2_cross, 2, p.cross_peer)
-    v_pass = remote(w2_cross, w2_cross, v_send.at[4], v_recv.at[4], p.sibling)
+
+    for r, source in enumerate((p.row, p.inner, p.cross, lax.rem(p.row + 2, rows))):
+        ln_scale[:, r * dim_local : (r + 1) * dim_local] = ln_all[:, aligned(source, dim_local)]
 
     def start(copy):
         copy.start()
@@ -129,17 +131,24 @@
         @pl.when(p.primary)
         def _():
             wb(k).wait_recv()
-            wc(k).start()
+            for c in wc_last if k == n_w - 1 else [wc(k)]:
+                c.start()
             wd(2, k).start()
-            wa(k).wait_recv()
-            wd(1, k).start()
             if k + AHEAD < n_w:
                 from_own(k + AHEAD, functools.partial(wa, k + AHEAD), start)
                 from_own(k + AHEAD, functools.partial(wd, 0, k + AHEAD), start)
 
+    def last_half(r, n):
+        return w_v.at[pl.ds(r * dim_local, dim_local), pl.ds((n_w - 1) * wide + n * (wide // 2), wide // 2)]
+
+    wc_last = [remote(last_half(2, n), last_half(3, n), wc_send.at[n_w - 1 + n], wc_recv.at[n_w - 1 + n], p.inner_peer) for n in range(2)]
+    wd_last = [remote(last_half(3, n), last_half(3, n), wd_send.at[n, n_w], wd_recv.at[n, n_w], p.sibling) for n in range(2)]
+
     def hand_over(k):
         @pl.when(p.primary)
         def _():
+            wa(k).wait_recv()
+            wd(1, k).start()
             wc(k).wait_recv()
             wd(3, k).start()
 
@@ -199,7 +208,7 @@
 
         @pl.when(k < n_q - 1)
         def _():
-            scale = qk_scale[pl.ds(k, 1), :]
+            scale = jnp.where(k == 0, qn_scale[...], kn_scale[...])
             for hd in range(heads):
                 part = slice(hd * head_dim, (hd + 1) * head_dim)
                 qkv_v[k, to, part] = layer_norm(z[:, part].astype(jnp.float32), scale).astype(jnp.bfloat16)
@@ -231,18 +240,13 @@
     def up_copy(rank, k, b):
         return pltpu.make_async_copy(up_v.at[b], h_hbm.at[aligned(rank, group), aligned(k - n_q + 1, wide)], up_sem.at[b])
 
+    def bias_of(here):
+        return jnp.where(p.primary, bias_own[:, here], bias_v[:, here])
+
     def up_chunk(k, carry):
         hand_over(k)
         receive(k)
-
-        @pl.when(jnp.logical_and(p.primary, k == n_w - 1))
-        def _():
-            for c in v_cross:
-                c.wait_recv()
-            v_pass.start()
-
-        here = aligned(k - n_q, wide)
-        bias = jnp.where(p.primary, bias_own[:, here], bias_v[:, here])
+        bias = bias_of(aligned(k - n_q, wide))
 
         def cell(rank, carry):
             b = lax.rem(rank, 2)
@@ -258,8 +262,52 @@
 
         return lax.fori_loop(0, rows, cell, carry)
 
+    def last_copy(rank, n):
+        to = pl.ds(wide + (n_up - 1) * wide + n * (wide // 2), wide // 2)
+        return pltpu.make_async_copy(last_v.at[n, lax.rem(rank, 2)], h_hbm.at[aligned(rank, group), to], last_sem.at[n, lax.rem(rank, 2)])
+
+    def last_chunk(n):
+        @pl.when(p.primary)
+        def _():
+            if n == 0:
+                wa(n_w - 1).wait_recv()
+                wd(1, n_w - 1).start()
+            wc_last[n].wait_recv()
+            wd_last[n].start()
+            if n == 0:
+                for c in v_cross:
+                    c.wait_recv()
+
+        @pl.when(jnp.logical_not(p.primary))
+        def _():
+            if n == 0:
+                for r in range(rows - 1):
+                    wd(r, n_w - 1).wait_recv()
+            wd_last[n].wait_recv()
+
+        first = (n_up - 1) * wide + n * (wide // 2)
+        bias = bias_of(pl.ds(first, wide // 2))
+        weight = pl.ds(n_q * wide + first, wide // 2)
+
+        def cell(rank, carry):
+            @pl.when(rank >= 2)
+            def _():
+                last_copy(rank - 2, n).wait()
+
+            m = jnp.dot(u_v[aligned(rank, group), :], w_v[:, weight], preferred_element_type=jnp.float32).astype(jnp.bfloat16).astype(jnp.float32) + bias
+            last_v[n, lax.rem(rank, 2)] = (0.5 * m * (1.0 + lax.erf(m * 0.5 ** 0.5))).astype(jnp.bfloat16)
+            last_copy(rank, n).start()
+            return carry
+
+        lax.fori_loop(0, rows, cell, 0)
+
     p.enter()
     xb.start()
+
+    @pl.when(jnp.logical_not(p.primary))
+    def _():
+        from_own(0, functools.partial(wb, 0), start)
+
     xa.start()
     bias_copy.start()
 
@@ -270,10 +318,6 @@
         for k in range(AHEAD):
             from_own(k, functools.partial(wa, k), start)
             from_own(k, functools.partial(wd, 0, k), start)
-
-    @pl.when(jnp.logical_not(p.primary))
-    def _():
-        from_own(0, functools.partial(wb, 0), start)
 
     xb.wait_recv()
     xc.start()
@@ -343,11 +387,15 @@
     pump(6)
     attend((rows - 1) * sub, sub)
     bias_copy.wait_recv()
-    lax.fori_loop(n_q, n_w, up_chunk, 0)
+    lax.fori_loop(n_q, n_w - 1, up_chunk, 0)
+    last_chunk(0)
+    last_chunk(1)
 
     for b in range(2):
         at_copy(b, b).wait()
         up_copy(b, n_q, b).wait()
+        for n in range(2):
+            last_copy(b, n).wait()
     for c in (xa, xb, xc, bias_copy):
         c.wait_send()
     for e in range(rows - 1):
@@ -358,10 +406,11 @@
     def _():
         for k in range(n_w):
             wa(k).wait_send()
-            wc(k).wait_send()
-            for r in range(rows):
+            if k < n_w - 1:
+                wc(k).wait_send()
+            for r in range(rows if k < n_w - 1 else rows - 1):
                 wd(r, k).wait_send()
-        for c in v_own + [v_pass]:
+        for c in v_own + wc_last + wd_last:
             c.wait_send()
 
     @pl.when(jnp.logical_not(p.primary))
@@ -370,14 +419,14 @@
             wb(k).wait_send()
         for c in v_cross:
             c.wait_send()
-        for c in v_own + [v_pass]:
+        for c in v_own:
             c.wait_recv()
 
 
-def stage_one(rows, chips, x_blk, ln_scale, qk_scale, b_up, wq, wu, w_o, w_down):
+def stage_one(rows, chips, x_blk, ln_scale, qn_scale, kn_scale, b_up, wq, wu, w_o, w_down):
     batch, patches, dim_local = x_blk.shape
     dim, wide = rows * dim_local, wq.shape[2]
-    heads = wide // qk_scale.shape[1]
+    heads = wide // qn_scale.shape[1]
     n_q, n_up = wq.shape[0], wu.shape[1] // wide
     n_w = n_q + n_up
     sub = batch // (2 * CORES * chips)
@@ -388,23 +437,23 @@
     h, _, w2_own, w2_cross = pl.pallas_call(
         functools.partial(stage_one_kernel, rows, chips, heads),
         out_shape=(jax.ShapeDtypeStruct((tokens, wide + n_up * wide), bf), jax.ShapeDtypeStruct((chips, rows - 1, sub, patches, dim_local), bf), w2, w2),
-        in_specs=[anyspec, vmspec, vmspec, vmspec] + [anyspec] * 4,
+        in_specs=[anyspec] + [vmspec] * 4 + [anyspec] * 4,
         out_specs=(anyspec,) * 4,
         scratch_shapes=[
             vm((tokens, dim), bf), vm((dim, n_w * wide), bf), vm((n_q, tokens, wide), bf), vm((2, patches, dim), bf),
-            vm((2, sub * patches, wide), bf), vm((2, patches, wide), bf), vm(b_up.shape, jnp.float32),
+            vm((2, sub * patches, wide), bf), vm((2, 2, sub * patches, wide // 2), bf), vm((2, patches, wide), bf), vm(b_up.shape, jnp.float32), vm(ln_scale.shape, jnp.float32),
             dma((3,)), dma((3,)), dma((rows - 1, 4)), dma((rows - 1, 4)), dma((2, rows)), dma((n_q + 1,)), dma, dma,
-            dma((n_w,)), dma((n_w,)), dma((n_w,)), dma((n_w,)), dma((n_w,)), dma((n_w,)), dma((rows, n_w)), dma((rows, n_w)), dma((2,)), dma((2,)), dma((5,)), dma((5,)),
+            dma((n_w,)), dma((n_w,)), dma((n_w,)), dma((n_w,)), dma((n_w + 1,)), dma((n_w + 1,)), dma((rows, n_w + 1)), dma((rows, n_w + 1)), dma((2,)), dma((2,)), dma((4,)), dma((4,)), dma((2, 2)),
         ],
         compiler_params=pltpu.CompilerParams(collective_id=0, has_side_effects=True, vmem_limit_bytes=VMEM_MAX),
         cost_estimate=pl.CostEstimate(flops=2 * tokens * dim * n_w * wide, bytes_accessed=1 << 27, transcendentals=0),
         name='stage_one',
-    )(x_blk, ln_scale, qk_scale, b_up, wq, wu, w_o, w_down)
+    )(x_blk, ln_scale, qn_scale, kn_scale, b_up, wq, wu, w_o, w_down)
     return h, w2_own, w2_cross
 
 
 def stage_two_kernel(rows, chips, x_hbm, h_hbm, w_o, w_down, w2_own, w2_cross, bias, out_hbm, h_v, w_v, ys_v, yt_v, x_v, rx_v, half_v, tot_v, t2_v, in_v, fin_v,
-                     ld_sem, wa_send, wa_recv, wc_send, wc_recv, wd_send, wd_recv, hf_send, hf_recv, x_send, x_recv, p_send, p_recv, t_send, t_recv,
+                     ld_sem, wa_send, wa_recv, wc_send, wc_recv, wd_send, wd_recv, wx_send, wx_recv, hf_send, hf_recv, x_send, x_recv, p_send, p_recv, t_send, t_recv,
                      i_send, i_recv, g_send, g_recv, s_send, s_recv, l_sem):
     p = Place(rows, chips)
     batch, patches, dim_local = x_hbm.shape
@@ -423,16 +472,19 @@
     wa = [two(c, 1, lambda s, d, n, c=c: remote(s, d, wa_send.at[c, n], wa_recv.at[c, n], p.inner_peer)) for c in range(CHUNKS)]
     wc = [remote(w2_cross.at[:, cols(c)], w_v.at[c, 3], wc_send.at[c], wc_recv.at[c], p.inner_peer) for c in range(CHUNKS)]
     wd = [{r: remote(w_v.at[c, r], w_v.at[c, r], wd_send.at[c, r // 2], wd_recv.at[c, r // 2], p.sibling) for r in (1, 3)} for c in range(CHUNKS)]
+    wx = [remote(w2_cross.at[:, cols(c)], w_v.at[c, 2], wx_send.at[c], wx_recv.at[c], p.sibling) for c in range(CHUNKS)]
     own_primary = [two(c, 0, lambda s, d, n, c=c: pltpu.make_async_copy(s, d, ld_sem.at[2 * c + n])) for c in range(CHUNKS)]
     own_other = [pltpu.make_async_copy(w2_own.at[:, cols(c)], w_v.at[c, 0], ld_sem.at[2 * c]) for c in range(CHUNKS)]
     cross_load = [pltpu.make_async_copy(w2_cross.at[:, cols(c)], w_v.at[c, 2], ld_sem.at[2 * CHUNKS + c]) for c in range(CHUNKS)]
-    h_copy = pltpu.make_async_copy(h_hbm, h_v, ld_sem.at[3 * CHUNKS])
+    def h_copy(rank):
+        return pltpu.make_async_copy(h_hbm.at[aligned(rank, group), :], h_v.at[aligned(rank, group), :], ld_sem.at[5 * CHUNKS + rank])
+
 
     def images(side, dx):
         return p.first_image(p.half if side == 0 else 1 - p.half, dx, p.core, batch)
 
     fin_load = [
-        [pltpu.make_async_copy(x_hbm.at[pl.ds(images(side, 0), sub), :, cols(c)], fin_v.at[side, c], ld_sem.at[3 * CHUNKS + 1 + side * CHUNKS + c]) for c in range(CHUNKS)]
+        [pltpu.make_async_copy(x_hbm.at[pl.ds(images(side, 0), sub), :, cols(c)], fin_v.at[side, c], ld_sem.at[3 * CHUNKS + side * CHUNKS + c]) for c in range(CHUNKS)]
         for side in (0, 1)
     ]
 
@@ -478,7 +530,17 @@
         return jnp.dot(h_v[aligned(rank, group), :], w_v[c, r], preferred_element_type=jnp.float32).astype(jnp.bfloat16).reshape(sub, patches, cw)
 
     def received(c, r):
-        if r in (1, 3):
+        if r == 2:
+
+            @pl.when(p.primary)
+            def _():
+                cross_load[c].wait()
+
+            @pl.when(jnp.logical_not(p.primary))
+            def _():
+                wx[c].wait_recv()
+
+        elif r:
 
             @pl.when(jnp.logical_not(p.primary))
             def _():
@@ -540,6 +602,8 @@
 
         def cell(n, carry):
             rank = far_rank - n
+            if u == 0:
+                h_copy(rank).wait()
             x_v[s, rank] = dot(rank, c, r)
 
             @pl.when(n == 0)
@@ -617,18 +681,26 @@
         g_copy(side, c, 3).wait_recv()
         s_copy(side, c, 3).start()
 
-    h_copy.start()
-    for c in range(CHUNKS):
-        cross_load[c].start()
-
+    def own_load(c, act):
         @pl.when(p.primary)
-        def _(c=c):
+        def _():
             for copy in own_primary[c]:
-                copy.start()
+                act(copy)
 
         @pl.when(jnp.logical_not(p.primary))
-        def _(c=c):
-            own_other[c].start()
+        def _():
+            act(own_other[c])
+
+    h_copy(far_rank).start()
+    own_load(1, lambda copy: copy.start())
+    for rank in reversed(range(far_rank)):
+        h_copy(rank).start()
+    own_load(0, lambda copy: copy.start())
+
+    @pl.when(p.primary)
+    def _():
+        for c in reversed(range(CHUNKS)):
+            cross_load[c].start()
 
     for side in (0, 1):
         for c in range(CHUNKS):
@@ -637,56 +709,44 @@
 
     @pl.when(p.primary)
     def _():
-        for copy in [wc[1], wc[0]] + wa[0] + wa[1]:
+        for copy in [wx[1], wx[0]] + wc + wa[0] + wa[1]:
             copy.start()
 
-    h_copy.wait()
-    for c in range(CHUNKS):
-
-        @pl.when(p.primary)
-        def _(c=c):
-            for copy in own_primary[c]:
-                copy.wait()
-
-        @pl.when(jnp.logical_not(p.primary))
-        def _(c=c):
-            own_other[c].wait()
-
-        cross_load[c].wait()
-
-    cross_part(0, 2)
+    own_load(1, lambda copy: copy.wait())
     compute(0, 1, 0)
     compute(1, 1, 2)
     mid(0)
+    cross_part(0, 2)
     mid(1)
+    fetch_far(0)
     reduce(0, 1, 0)
+    compute(2, 0, 3)
+    reduce(1, 1, 1, t_copy)
+    own_load(0, lambda copy: copy.wait())
+    pair_part(3, 0, 0)
+    mid(2)
+    home(0, 0, 3)
     fetch_far(1)
-    pair_part(2, 0, 0)
-    reduce(1, 1, 1, t_copy)
     cross_part(1, 3)
-    fetch_far(0)
-    compute(3, 0, 3)
     home(0, 1)
-    home(0, 0, 2)
-    mid(3)
-    near(0, 1)
-    near(0, 0)
-    reduce(3, 0, 1, t_copy)
     fetch_inner(0)
     compute(4, 0, 1)
+    near(0, 0)
+    reduce(2, 0, 1, t_copy)
+    mid(4)
+    fetch_inner(1)
+    pair_part(5, 1, 1)
+    reduce(4, 0, 0)
+    near(0, 1)
+    pass_on(0)
+    reduce(5, 1, 2, i_copy)
+    home(1, 0)
+    home(1, 1)
+    far(0, 0)
     far(0, 1)
-    mid(4)
-    far(0, 0)
-    reduce(4, 0, 0)
-    fetch_inner(1)
-    pass_on(0)
-    pair_part(5, 1, 1)
-    home(1, 0)
-    reduce(5, 1, 2, i_copy)
     near(1, 0)
-    home(1, 1)
+    near(1, 1)
     far(1, 0)
-    near(1, 1)
     far(1, 1)
 
     for c in range(CHUNKS):
@@ -709,6 +769,7 @@
     def _():
         for c in range(CHUNKS):
             wc[c].wait_send()
+            wx[c].wait_send()
             for copy in wa[c]:
                 copy.wait_send()
             for r in (1, 3):
@@ -732,7 +793,7 @@
             vm(h.shape, bf), vm((CHUNKS, rows, k_dim, cw), bf), vm((CHUNKS, chips) + piece, bf), vm((CHUNKS, chips) + piece, bf), vm((3, chips) + piece, bf),
             vm((units, 2) + piece, bf), vm((units, 2, patches, cw), bf), vm((3, CHUNKS) + piece, bf), vm((CHUNKS,) + piece, bf), vm((CHUNKS,) + piece, bf),
             vm((2, CHUNKS) + piece, bf),
-            dma((5 * CHUNKS + 1,)), dma((CHUNKS, 2)), dma((CHUNKS, 2)), dma((CHUNKS,)), dma((CHUNKS,)), dma((CHUNKS, 2)), dma((CHUNKS, 2)),
+            dma((5 * CHUNKS + rows,)), dma((CHUNKS, 2)), dma((CHUNKS, 2)), dma((CHUNKS,)), dma((CHUNKS,)), dma((CHUNKS, 2)), dma((CHUNKS, 2)), dma((CHUNKS,)), dma((CHUNKS,)),
             dma((units, 2)), dma((units, 2)), dma((units, 2)), dma((units, 2)), dma((CHUNKS, chips)), dma((CHUNKS, chips)), dma((CHUNKS,)), dma((CHUNKS,)),
             dma((CHUNKS,)), dma((CHUNKS,)), dma((2, CHUNKS, 4)), dma((2, CHUNKS, 4)), dma((2, CHUNKS, 4)), dma((2, CHUNKS, 4)), dma((2, CHUNKS)),
         ],
@@ -742,18 +803,42 @@
     )(x_blk, h, w_o, w_down, w2_own, w2_cross, b_out.reshape(1, dim_local))
 
 
+def copy_kernel(src, dst, held, in_sem, out_sem):
+    count = in_sem.shape[0]
+    step = src.shape[0] // count
+    loads = [pltpu.make_async_copy(src.at[pl.ds(n * step, step)], held.at[pl.ds(n * step, step)], in_sem.at[n]) for n in range(count)]
+    stores = [pltpu.make_async_copy(held.at[pl.ds(n * step, step)], dst.at[pl.ds(n * step, step)], out_sem.at[n]) for n in range(count)]
+    for c in loads:
+        c.start()
+    for n in range(count):
+        loads[n].wait()
+        stores[n].start()
+    for c in stores:
+        c.wait()
+
+
+def copy_out(array):
+    count = 16
+    return pl.pallas_call(
+        copy_kernel,
+        out_shape=jax.ShapeDtypeStruct(array.shape, array.dtype),
+        in_specs=[pl.BlockSpec(memory_space=pl.ANY)],
+        out_specs=pl.BlockSpec(memory_space=pl.ANY),
+        scratch_shapes=[pltpu.VMEM(array.shape, array.dtype), pltpu.SemaphoreType.DMA((count,)), pltpu.SemaphoreType.DMA((count,))],
+        compiler_params=pltpu.CompilerParams(vmem_limit_bytes=VMEM_MAX),
+        name='copy_out',
+    )(array)
+
+
 def solution(mesh):
     rows, cols = mesh.shape['m1'], mesh.shape['m2']
     chips = cols // CORES
     assert rows == 4 and chips == 4
 
     def local_layer(x_blk, ln_scale, qn_scale, kn_scale, w_qkv, w_up, b_up, w_o, w_down, b_out):
-        dim_local = x_blk.shape[2]
-        row = lax.axis_index('m1')
-        inner, cross = row + 1 - 2 * lax.rem(row, 2), rows - 1 - row
-        seen = (row, inner, cross, lax.rem(row + 2, rows))
-        scale = jnp.concatenate([lax.dynamic_slice_in_dim(ln_scale, r * dim_local, dim_local) for r in seen])
-        h, w2_own, w2_cross = stage_one(rows, chips, x_blk, scale[None], jnp.stack([qn_scale, kn_scale]), b_up[None], w_qkv.transpose(1, 0, 2), w_up, w_o, w_down)
-        return stage_two(rows, chips, x_blk, h, w_o, w_down, w2_own, w2_cross, b_out)
+        h, w2_own, w2_cross = stage_one(
+            rows, chips, x_blk, ln_scale[None], qn_scale[None], kn_scale[None], b_up[None], w_qkv.transpose(1, 0, 2), w_up, w_o, w_down
+        )
+        return copy_out(stage_two(rows, chips, x_blk, h, w_o, w_down, w2_own, w2_cross, b_out))
 
     return jax.shard_map(local_layer, mesh=mesh, in_specs=(P('dp', None, 'm1'), P(), P(), P(), P('m1', None, 'm2'), P('m1', 'm2'), P('m2'), P('m2', 'm1'), P('m2', 'm1'), P('m1')), out_specs=P('dp', None, 'm1'), check_vma=False)

time: 427 us -> 402 us (0.941)
  local copies, waits for them, and re-layouts: 14.6 us -> 0 us
  Pallas kernels: 410 us -> 402 us
    pallas_call x1, Pallas kernels: 203 us -> 184 us  [stage_two(): pl.pallas_call(functools.partial(stage_two_kernel, rows, chips), out_shap...]
    unnamed x1 -> x0, local copies, waits for them, and re-layouts: 13.9 us -> none
    pallas_call x0 -> x1, Pallas kernels: none -> 12 us  [copy_out(): pl.pallas_call(copy_kernel, out_shape=jax.ShapeDtypeStruct(array.shape, a...]
where the time goes in v3:
time: 402 us
  Pallas kernels  402 us (100%)
    pallas_call x1, Pallas kernels, stage_one(): pl.pallas_call(functools.partial(stage_one_kernel, rows, chips, heads), o...  205 us
    pallas_call x1, Pallas kernels, stage_two(): pl.pallas_call(functools.partial(stage_two_kernel, rows, chips), out_shap...  184 us
    pallas_call x1, Pallas kernels, copy_out(): pl.pallas_call(copy_kernel, out_shape=jax.ShapeDtypeStruct(array.shape, a...  12 us

profile of v3, /device:TPU:97, one launch (start us, length us, event | category | flops | bytes accessed | tf_op | source)
XLA Modules:
  0.0 401.7 jit_solution(10975736023226148381)
XLA Ops:
  0.0 205.5 %stage_one.1 = (bf16[2048,2560]{1,0:T(8,128)(2,1)}, bf16[4,3,2,256,1024]{4,3,2,1,0:T(8,128)(2,1)}, bf16[2560,1024]{1,0:T(8,128)(2,1)}, bf16[2560,1024]{1,0:T(8,128)(2,1)}) custom-call(bf16[32,256,1024]{2,1,0:T(8,128)(2,1)} %x_hbm.3, f32[1,4096]{1,0:T(1,128)} %bitcast.7, f32[1,128]{1,0:T(1,128)} %bitcast.10, f32[1,128]{1,0:T(1,128)} %bitcast.11, ...), custom_call_target="tpu_custom_call" | custom-call | flops 60129542144 | bytes 134217728 | tf_op jit(solution)/shard_map/stage_one/pallas_call | solution.py:437
  205.5 184.1 %stage_two.1.src = bf16[32,256,1024]{2,1,0:T(8,128)(2,1)} custom-call(bf16[32,256,1024]{2,1,0:T(8,128)(2,1)} %x_hbm.3, bf16[2048,2560]{1,0:T(8,128)(2,1)} %get-tuple-element.8.h_hbm, bf16[512,1024]{1,0:T(8,128)(2,1)} %w_o.3, bf16[2048,1024]{1,0:T(8,128)(2,1)} %w_down.3, bf16[2560,1024]{1,0:T(8,128)(2,1)} %get-tuple-element.9.w2_own, ...), custom_call_target="tpu_custom_call" | custom-call | flops 42949672960 | bytes 134217728 | tf_op jit(solution)/shard_map/stage_two/pallas_call | solution.py:787
  389.6 12.0 %copy_out.1 = bf16[32,256,1024]{2,1,0:T(8,128)(2,1)} custom-call(bf16[32,256,1024]{2,1,0:T(8,128)(2,1)} %stage_two.1.src), custom_call_target="tpu_custom_call" | custom-call | tf_op jit(solution)/shard_map/copy_out/pallas_call | solution.py:822

commit v4 on v3

--- a/solution.py
+++ b/solution.py
@@ -11,8 +11,21 @@
 CORES = 2
 LINES = 16
 LANES = 128
-AHEAD = 2
-CHUNKS = 2
+NEXT_CHUNK = (2, 3, 4, None, 5, 6, None)
+CHUNKS = 4
+X_SLOTS = 6
+SEND_SLOTS = 3
+PLAN = (
+    ('send', 1, 2), ('part', 3, 2, 0), ('part', 2, 0, 1), ('mid', 0), ('mid', 1), ('part', 3, 0, 2), ('sum', 3, 2, 0), ('pass', 2, 3),
+    ('send', 0, 2), ('pair', 1, 0, 3), ('sum', 2, 0, 1), ('mid', 2), ('part', 2, 2, 4), ('send', 2, 3), ('sum', 3, 0, 2), ('home', 0, 3),
+    ('pair', 0, 0, 5), ('mid', 4), ('pass', 2, 1), ('home', 0, 0, 5), ('pass', 0, 3), ('send', 0, 3), ('pair', 2, 1, 6), ('pass', 1, 3),
+    ('near', 0, 0), ('home', 0, 1, 3), ('pass', 3, 3), ('pass', 0, 1), ('sum', 2, 1, 6), ('sum', 2, 2, 4), ('send', 3, 3), ('near', 0, 3),
+    ('pair', 0, 1, 7), ('pass', 3, 1), ('home', 0, 2), ('far', 0, 0), ('sum', 0, 1, 7), ('far', 0, 3), ('near', 0, 1), ('send', 1, 3),
+    ('pass', 1, 1), ('near', 0, 2), ('pair', 3, 1, 8), ('home', 1, 0), ('far', 0, 1), ('sum', 3, 1, 8), ('far', 0, 2), ('home', 1, 2),
+    ('pair', 1, 1, 9), ('near', 1, 2), ('near', 1, 0), ('sum', 1, 1, 9), ('home', 1, 3), ('home', 1, 1), ('near', 1, 3), ('near', 1, 1),
+    ('far', 1, 3), ('far', 1, 0), ('far', 1, 2), ('far', 1, 1),
+)
+INNER_ORDER = ((2, 3), (1, 3), (0, 3), (2, 1), (3, 3), (0, 1), (3, 1), (1, 1))
 VMEM_MAX = 67043328
 MESH = pl.DeviceIdType.MESH
 
@@ -134,9 +147,10 @@
             for c in wc_last if k == n_w - 1 else [wc(k)]:
                 c.start()
             wd(2, k).start()
-            if k + AHEAD < n_w:
-                from_own(k + AHEAD, functools.partial(wa, k + AHEAD), start)
-                from_own(k + AHEAD, functools.partial(wd, 0, k + AHEAD), start)
+            later = NEXT_CHUNK[k]
+            if later is not None:
+                from_own(later, functools.partial(wa, later), start)
+                from_own(later, functools.partial(wd, 0, later), start)
 
     def last_half(r, n):
         return w_v.at[pl.ds(r * dim_local, dim_local), pl.ds((n_w - 1) * wide + n * (wide // 2), wide // 2)]
@@ -274,9 +288,6 @@
                 wd(1, n_w - 1).start()
             wc_last[n].wait_recv()
             wd_last[n].start()
-            if n == 0:
-                for c in v_cross:
-                    c.wait_recv()
 
         @pl.when(jnp.logical_not(p.primary))
         def _():
@@ -315,7 +326,7 @@
     def _():
         for c in own_copies:
             c.start()
-        for k in range(AHEAD):
+        for k in range(NEXT_CHUNK[0]):
             from_own(k, functools.partial(wa, k), start)
             from_own(k, functools.partial(wd, 0, k), start)
 
@@ -412,6 +423,8 @@
                 wd(r, k).wait_send()
         for c in v_own + wc_last + wd_last:
             c.wait_send()
+        for c in v_cross:
+            c.wait_recv()
 
     @pl.when(jnp.logical_not(p.primary))
     def _():
@@ -462,6 +475,9 @@
     ko, kd = w_o.shape[0], w_down.shape[0]
     cw = dim_local // CHUNKS
     far_rank = rows - 1
+    sends = [step[1:] for step in PLAN if step[0] == 'send']
+    units = [step for step in PLAN if step[0] in ('part', 'pair')]
+    late = [step[1] for step in PLAN if step[0] == 'sum' and step[2] == 2]
 
     def cols(c):
         return pl.ds(c * cw, cw)
@@ -488,16 +504,16 @@
         for side in (0, 1)
     ]
 
-    def p_copy(c, rank):
-        return remote(ys_v.at[c, rank], yt_v.at[c, rank], p_send.at[c, rank], p_recv.at[c, rank], p.cross_peer)
+    def p_copy(n, rank):
+        return remote(ys_v.at[n % SEND_SLOTS, rank], yt_v.at[n, rank], p_send.at[n, rank], p_recv.at[n, rank], p.cross_peer)
 
     def half_copy(u, k):
         who = p.right_peer if k == 0 else p.left_peer
-        return remote(x_v.at[u % 3, far_rank, k], half_v.at[u, k], hf_send.at[u, k], hf_recv.at[u, k], who)
+        return remote(x_v.at[u % X_SLOTS, far_rank, k], half_v.at[u, k], hf_send.at[u, k], hf_recv.at[u, k], who)
 
     def x_copy(u, k):
         who = p.right_peer if k == 0 else p.left_peer
-        return remote(x_v.at[u % 3, 2 - k], rx_v.at[u, k], x_send.at[u, k], x_recv.at[u, k], who)
+        return remote(x_v.at[u % X_SLOTS, 2 - k], rx_v.at[u, k], x_send.at[u, k], x_recv.at[u, k], who)
 
     def t_copy(c):
         return remote(tot_v.at[1, c], t2_v.at[c], t_send.at[c], t_recv.at[c], p.cross_peer)
@@ -529,8 +545,20 @@
     def dot(rank, c, r):
         return jnp.dot(h_v[aligned(rank, group), :], w_v[c, r], preferred_element_type=jnp.float32).astype(jnp.bfloat16).reshape(sub, patches, cw)
 
+    def own_load(c, act):
+        @pl.when(p.primary)
+        def _():
+            for copy in own_primary[c]:
+                act(copy)
+
+        @pl.when(jnp.logical_not(p.primary))
+        def _():
+            act(own_other[c])
+
     def received(c, r):
-        if r == 2:
+        if r == 0:
+            own_load(c, lambda copy: copy.wait())
+        elif r == 2:
 
             @pl.when(p.primary)
             def _():
@@ -548,37 +576,44 @@
 
     def cross_part(c, r):
         received(c, r)
+        number = sends.index((c, r))
+        if number >= SEND_SLOTS:
+            for rank in range(chips):
+                p_copy(number - SEND_SLOTS, rank).wait_send()
 
         def cell(n, carry):
             rank = far_rank - n
-            ys_v[c, rank] = dot(rank, c, r)
-            p_copy(c, rank).start()
+            if number == 0:
+                h_copy(rank).wait()
+            ys_v[number % SEND_SLOTS, rank] = dot(rank, c, r)
+            p_copy(number, rank).start()
             return carry
 
         lax.fori_loop(0, chips, cell, 0)
 
     def reuse(u):
-        if u >= 3:
+        if u >= X_SLOTS:
             for k in range(2):
-                half_copy(u - 3, k).wait_send()
-                x_copy(u - 3, k).wait_send()
+                half_copy(u - X_SLOTS, k).wait_send()
+                x_copy(u - X_SLOTS, k).wait_send()
 
     def mid_one(u, k):
         half_copy(u, k).wait_recv()
-        s = u % 3
+        s = u % X_SLOTS
         x_v[s, 2 - k, k] = add(x_v[s, 2 - k, k], half_v[u, k]).astype(jnp.bfloat16)
         x_copy(u, k).start()
 
     def pair_part(u, c, r):
         reuse(u)
-        s = u % 3
+        s = u % X_SLOTS
         received(c, r)
+        number = sends.index((c, r + 2))
 
         def cell(n, carry):
             rank = far_rank - n
             part = dot(rank, c, r)
-            p_copy(c, rank).wait_recv()
-            x_v[s, rank] = add(part, yt_v[c, rank]).astype(jnp.bfloat16)
+            p_copy(number, rank).wait_recv()
+            x_v[s, rank] = add(part, yt_v[number, rank]).astype(jnp.bfloat16)
 
             @pl.when(n == 0)
             def _():
@@ -597,13 +632,11 @@
 
     def compute(u, c, r):
         reuse(u)
-        s = u % 3
+        s = u % X_SLOTS
         received(c, r)
 
         def cell(n, carry):
             rank = far_rank - n
-            if u == 0:
-                h_copy(rank).wait()
             x_v[s, rank] = dot(rank, c, r)
 
             @pl.when(n == 0)
@@ -620,7 +653,7 @@
         mid_one(u, 1)
 
     def total(u, n):
-        s = u % 3
+        s = u % X_SLOTS
         return add(x_v[s, 0, n], rx_v[u, 0, n]) + rx_v[u, 1, n].astype(jnp.float32)
 
     def arrived(u):
@@ -646,12 +679,6 @@
             for copy in wa[c]:
                 copy.wait_recv()
             wd[c][1].start()
-
-    def pass_on(c):
-        t_copy(c).wait_recv()
-        for n in range(sub):
-            tot_v[2, c, n] = add(tot_v[0, c, n], t2_v[c, n]).astype(jnp.bfloat16)
-        i_copy(c).start()
 
     def home(side, c, u=None):
         if u is None:
@@ -681,26 +708,17 @@
         g_copy(side, c, 3).wait_recv()
         s_copy(side, c, 3).start()
 
-    def own_load(c, act):
-        @pl.when(p.primary)
-        def _():
-            for copy in own_primary[c]:
-                act(copy)
-
-        @pl.when(jnp.logical_not(p.primary))
-        def _():
-            act(own_other[c])
-
-    h_copy(far_rank).start()
-    own_load(1, lambda copy: copy.start())
-    for rank in reversed(range(far_rank)):
+    for rank in reversed(range(chips)):
         h_copy(rank).start()
-    own_load(0, lambda copy: copy.start())
-
-    @pl.when(p.primary)
-    def _():
-        for c in reversed(range(CHUNKS)):
-            cross_load[c].start()
+    needs = [step[1:3] for step in PLAN if step[0] in ('send', 'part', 'pair')]
+    for c, r in needs:
+        if r == 0:
+            own_load(c, lambda copy: copy.start())
+        elif r == 2:
+
+            @pl.when(p.primary)
+            def _(c=c):
+                cross_load[c].start()
 
     for side in (0, 1):
         for c in range(CHUNKS):
@@ -709,45 +727,34 @@
 
     @pl.when(p.primary)
     def _():
-        for copy in [wx[1], wx[0]] + wc + wa[0] + wa[1]:
-            copy.start()
-
-    own_load(1, lambda copy: copy.wait())
-    compute(0, 1, 0)
-    compute(1, 1, 2)
-    mid(0)
-    cross_part(0, 2)
-    mid(1)
-    fetch_far(0)
-    reduce(0, 1, 0)
-    compute(2, 0, 3)
-    reduce(1, 1, 1, t_copy)
-    own_load(0, lambda copy: copy.wait())
-    pair_part(3, 0, 0)
-    mid(2)
-    home(0, 0, 3)
-    fetch_far(1)
-    cross_part(1, 3)
-    home(0, 1)
-    fetch_inner(0)
-    compute(4, 0, 1)
-    near(0, 0)
-    reduce(2, 0, 1, t_copy)
-    mid(4)
-    fetch_inner(1)
-    pair_part(5, 1, 1)
-    reduce(4, 0, 0)
-    near(0, 1)
-    pass_on(0)
-    reduce(5, 1, 2, i_copy)
-    home(1, 0)
-    home(1, 1)
-    far(0, 0)
-    far(0, 1)
-    near(1, 0)
-    near(1, 1)
-    far(1, 0)
-    far(1, 1)
+        for c, r in needs:
+            if r == 2:
+                wx[c].start()
+        for c, r in INNER_ORDER:
+            for copy in [wc[c]] if r == 3 else wa[c]:
+                copy.start()
+
+    assert PLAN[0][0] == 'send'
+    for step, *of in PLAN:
+        if step == 'send':
+            cross_part(*of)
+        elif step == 'part':
+            compute(of[2], of[0], of[1])
+        elif step == 'pair':
+            pair_part(of[2], of[0], of[1])
+        elif step == 'mid':
+            mid(*of)
+        elif step == 'sum':
+            c, r, u = of
+            reduce(u, c, {0: 0, 2: 1, 1: 2}[r], {0: None, 2: t_copy, 1: i_copy}[r])
+        elif step == 'pass':
+            (fetch_far if of[1] == 3 else fetch_inner)(of[0])
+        elif step == 'home':
+            home(*of)
+        elif step == 'near':
+            near(*of)
+        else:
+            far(*of)
 
     for c in range(CHUNKS):
         for side in (0, 1):
@@ -756,11 +763,13 @@
                 s_copy(side, c, k).wait_send()
                 g_copy(side, c, k).wait_send()
             l_copy(side, c).wait()
-        t_copy(c).wait_send()
+        if c in late:
+            t_copy(c).wait_send()
         i_copy(c).wait_send()
+    for number in range(len(sends) - SEND_SLOTS, len(sends)):
         for rank in range(chips):
-            p_copy(c, rank).wait_send()
-    for u in (3, 4, 5):
+            p_copy(number, rank).wait_send()
+    for u in range(len(units) - X_SLOTS, len(units)):
         for k in range(2):
             half_copy(u, k).wait_send()
             x_copy(u, k).wait_send()
@@ -780,7 +789,8 @@
     batch, patches, dim_local = x_blk.shape
     sub = batch // (2 * CORES * chips)
     k_dim, cw = w2_own.shape[0], dim_local // CHUNKS
-    units = 3 * CHUNKS
+    units = sum(step[0] in ('part', 'pair') for step in PLAN)
+    sends = sum(step[0] == 'send' for step in PLAN)
     bf, vm, dma = jnp.bfloat16, pltpu.VMEM, pltpu.SemaphoreType.DMA
     piece = (sub, patches, cw)
     anyspec, vmspec = pl.BlockSpec(memory_space=pl.ANY), pl.BlockSpec(memory_space=pltpu.VMEM)
@@ -790,11 +800,11 @@
         in_specs=[anyspec] * 6 + [vmspec],
         out_specs=anyspec,
         scratch_shapes=[
-            vm(h.shape, bf), vm((CHUNKS, rows, k_dim, cw), bf), vm((CHUNKS, chips) + piece, bf), vm((CHUNKS, chips) + piece, bf), vm((3, chips) + piece, bf),
+            vm(h.shape, bf), vm((CHUNKS, rows, k_dim, cw), bf), vm((SEND_SLOTS, chips) + piece, bf), vm((sends, chips) + piece, bf), vm((X_SLOTS, chips) + piece, bf),
             vm((units, 2) + piece, bf), vm((units, 2, patches, cw), bf), vm((3, CHUNKS) + piece, bf), vm((CHUNKS,) + piece, bf), vm((CHUNKS,) + piece, bf),
             vm((2, CHUNKS) + piece, bf),
             dma((5 * CHUNKS + rows,)), dma((CHUNKS, 2)), dma((CHUNKS, 2)), dma((CHUNKS,)), dma((CHUNKS,)), dma((CHUNKS, 2)), dma((CHUNKS, 2)), dma((CHUNKS,)), dma((CHUNKS,)),
-            dma((units, 2)), dma((units, 2)), dma((units, 2)), dma((units, 2)), dma((CHUNKS, chips)), dma((CHUNKS, chips)), dma((CHUNKS,)), dma((CHUNKS,)),
+            dma((units, 2)), dma((units, 2)), dma((units, 2)), dma((units, 2)), dma((sends, chips)), dma((sends, chips)), dma((CHUNKS,)), dma((CHUNKS,)),
             dma((CHUNKS,)), dma((CHUNKS,)), dma((2, CHUNKS, 4)), dma((2, CHUNKS, 4)), dma((2, CHUNKS, 4)), dma((2, CHUNKS, 4)), dma((2, CHUNKS)),
         ],
         compiler_params=pltpu.CompilerParams(collective_id=1, has_side_effects=True, vmem_limit_bytes=VMEM_MAX),

time: 402 us -> 395 us (0.983)
  Pallas kernels: 402 us -> 395 us
    pallas_call x1, Pallas kernels: 205 us -> 201 us  [stage_one(): pl.pallas_call(functools.partial(stage_one_kernel, rows, chips, heads), o...]
where the time goes in v4:
time: 395 us
  Pallas kernels  395 us (100%)
    pallas_call x1, Pallas kernels, stage_one(): pl.pallas_call(functools.partial(stage_one_kernel, rows, chips, heads), o...  201 us
    pallas_call x1, Pallas kernels, stage_two(): pl.pallas_call(functools.partial(stage_two_kernel, rows, chips), out_shap...  182 us
    pallas_call x1, Pallas kernels, copy_out(): pl.pallas_call(copy_kernel, out_shape=jax.ShapeDtypeStruct(array.shape, a...  12 us

profile of v4, /device:TPU:97, one launch (start us, length us, event | category | flops | bytes accessed | tf_op | source)
XLA Modules:
  0.0 394.9 jit_solution(9982086663385668608)
XLA Ops:
  0.0 200.9 %stage_one.1 = (bf16[2048,2560]{1,0:T(8,128)(2,1)}, bf16[4,3,2,256,1024]{4,3,2,1,0:T(8,128)(2,1)}, bf16[2560,1024]{1,0:T(8,128)(2,1)}, bf16[2560,1024]{1,0:T(8,128)(2,1)}) custom-call(bf16[32,256,1024]{2,1,0:T(8,128)(2,1)} %x_hbm.3, f32[1,4096]{1,0:T(1,128)} %bitcast.7, f32[1,128]{1,0:T(1,128)} %bitcast.10, f32[1,128]{1,0:T(1,128)} %bitcast.11, ...), custom_call_target="tpu_custom_call" | custom-call | flops 60129542144 | bytes 134217728 | tf_op jit(solution)/shard_map/stage_one/pallas_call | solution.py:450
  200.9 181.8 %stage_two.1.src = bf16[32,256,1024]{2,1,0:T(8,128)(2,1)} custom-call(bf16[32,256,1024]{2,1,0:T(8,128)(2,1)} %x_hbm.3, bf16[2048,2560]{1,0:T(8,128)(2,1)} %get-tuple-element.8.h_hbm, bf16[512,1024]{1,0:T(8,128)(2,1)} %w_o.3, bf16[2048,1024]{1,0:T(8,128)(2,1)} %w_down.3, bf16[2560,1024]{1,0:T(8,128)(2,1)} %get-tuple-element.9.w2_own, ...), custom_call_target="tpu_custom_call" | custom-call | flops 42949672960 | bytes 134217728 | tf_op jit(solution)/shard_map/stage_two/pallas_call | solution.py:797
  382.7 12.0 %copy_out.1 = bf16[32,256,1024]{2,1,0:T(8,128)(2,1)} custom-call(bf16[32,256,1024]{2,1,0:T(8,128)(2,1)} %stage_two.1.src), custom_call_target="tpu_custom_call" | custom-call | tf_op jit(solution)/shard_map/copy_out/pallas_call | solution.py:832

commit v5 on v4

--- a/solution.py
+++ b/solution.py
@@ -342,10 +342,10 @@
         for c in v_cross:
             c.start()
 
+    pump(0)
     xa.wait_recv()
     ag(1, 0).start()
     ag(1, 1).start()
-    pump(0)
     xc.wait_recv()
     ag(2, 0).start()
     ag(2, 1).start()
@@ -382,11 +382,11 @@
     cells(1, lambda n: (n, n + 1))
     forward(2)
     normalize((1, 2))
+    pump(3)
+    cells((n_q - 1) * 2, lambda n: (1 + lax.rem(n, 2), n // 2))
     hand_over(2)
-    pump(3)
     receive(2)
-    early = (n_q - 1) * 2
-    cells(early + rows - 1, lambda n: (jnp.where(n < early, 1 + lax.rem(n, 2), n - early), jnp.where(n < early, n // 2, n_q - 1)))
+    cells(rows - 1, lambda n: (n, n_q - 1))
     pump(4)
     attend(0, (rows - 1) * sub)
     pump(5)

time: 395 us -> 395 us (level)
  no operation moved by 1% of the time
where the time goes in v5:
time: 395 us; the launch traced here: 394 us
  Pallas kernels  394 us (100%)
    pallas_call x1, Pallas kernels, stage_one(): pl.pallas_call(functools.partial(stage_one_kernel, rows, chips, heads), o...  200 us
    pallas_call x1, Pallas kernels, stage_two(): pl.pallas_call(functools.partial(stage_two_kernel, rows, chips), out_shap...  182 us
    pallas_call x1, Pallas kernels, copy_out(): pl.pallas_call(copy_kernel, out_shape=jax.ShapeDtypeStruct(array.shape, a...  12 us

profile of v5, /device:TPU:97, one launch (start us, length us, event | category | flops | bytes accessed | tf_op | source)
XLA Modules:
  0.0 394.4 jit_solution(9793278589537436603)
XLA Ops:
  0.0 200.2 %stage_one.1 = (bf16[2048,2560]{1,0:T(8,128)(2,1)}, bf16[4,3,2,256,1024]{4,3,2,1,0:T(8,128)(2,1)}, bf16[2560,1024]{1,0:T(8,128)(2,1)}, bf16[2560,1024]{1,0:T(8,128)(2,1)}) custom-call(bf16[32,256,1024]{2,1,0:T(8,128)(2,1)} %x_hbm.3, f32[1,4096]{1,0:T(1,128)} %bitcast.7, f32[1,128]{1,0:T(1,128)} %bitcast.10, f32[1,128]{1,0:T(1,128)} %bitcast.11, ...), custom_call_target="tpu_custom_call" | custom-call | flops 60129542144 | bytes 134217728 | tf_op jit(solution)/shard_map/stage_one/pallas_call | solution.py:450
  200.2 182.0 %stage_two.1.src = bf16[32,256,1024]{2,1,0:T(8,128)(2,1)} custom-call(bf16[32,256,1024]{2,1,0:T(8,128)(2,1)} %x_hbm.3, bf16[2048,2560]{1,0:T(8,128)(2,1)} %get-tuple-element.8.h_hbm, bf16[512,1024]{1,0:T(8,128)(2,1)} %w_o.3, bf16[2048,1024]{1,0:T(8,128)(2,1)} %w_down.3, bf16[2560,1024]{1,0:T(8,128)(2,1)} %get-tuple-element.9.w2_own, ...), custom_call_target="tpu_custom_call" | custom-call | flops 42949672960 | bytes 134217728 | tf_op jit(solution)/shard_map/stage_two/pallas_call | solution.py:797
  382.2 12.0 %copy_out.1 = bf16[32,256,1024]{2,1,0:T(8,128)(2,1)} custom-call(bf16[32,256,1024]{2,1,0:T(8,128)(2,1)} %stage_two.1.src), custom_call_target="tpu_custom_call" | custom-call | tf_op jit(solution)/shard_map/copy_out/pallas_call | solution.py:832
